TPU v7x, 32 devices: a 4x2x2 block of a 4x4x8 slice. The times are simulated.
32 devices in a mesh: dp: 4 (over y, z), ep: 8 (over x, core).
Axes of the slice: x: 4, y: 2, z: 2, core: 2. Of those that a mesh axis runs over, the one named last changes fastest.
The devices are a block of a 4x4x8 slice.
Arguments:
- tokens: bfloat16 [96, 128, 2048], P(('dp', 'ep')), parts along dimension 0
- w_query: bfloat16 [2048, 32, 128], P('ep')
- w_key: bfloat16 [2048, 32, 128], P('ep')
- w_value: bfloat16 [2048, 32, 128], P('ep')
- w_out: bfloat16 [4096, 2048], P('ep')
- w_router: float32 [2048, 128], replicated
- w_one: bfloat16 [128, 2048, 768], P('ep')
- w_three: bfloat16 [128, 2048, 768], P('ep')
- w_two: bfloat16 [128, 768, 2048], P('ep')
- expert_ids: int32 [96, 128, 8], P(('dp', 'ep')), parts along dimension 0
Outputs:
- output: bfloat16 [96, 128, 2048], P(('dp', 'ep')), parts along dimension 0
There are 4 independent parts. A program takes and returns all parts, laid end to end along the dimension named above; an argument that names none is the same for every part.
All inputs are finite; a program needn't handle non-finite values.
Results may differ from a plain program's by a relative error of at most 0.0104012.
Values are sent between devices in bfloat16 or wider.
A program may use at most 768 MiB of HBM per device.

v0:
```python
import jax
import jax.numpy as jnp
from jax import lax
from jax.sharding import PartitionSpec as P

EPS = 1e-6


def rms_norm(vals):
    wide = vals.astype(jnp.float32)
    return wide * lax.rsqrt(jnp.mean(wide * wide, axis=-1, keepdims=True) + EPS)


def attention_layer(tokens, w_query, w_key, w_value, w_out):
    seq_count = tokens.shape[0]
    seq_len = tokens.shape[1]
    head_dim = w_query.shape[2]
    normed = rms_norm(tokens).astype(jnp.bfloat16)
    query = jnp.einsum('bsd,dhk->bshk', normed, w_query, preferred_element_type=jnp.float32).astype(jnp.bfloat16)
    keys = jnp.einsum('bsd,dhk->bshk', normed, w_key, preferred_element_type=jnp.float32).astype(jnp.bfloat16)
    values = jnp.einsum('bsd,dhk->bshk', normed, w_value, preferred_element_type=jnp.float32).astype(jnp.bfloat16)
    scores = jnp.einsum('bqhk,bshk->bhqs', query, keys, preferred_element_type=jnp.float32) * head_dim ** -0.5
    causal = lax.broadcasted_iota(jnp.int32, (seq_len, seq_len), 0) >= lax.broadcasted_iota(jnp.int32, (seq_len, seq_len), 1)
    attn_weights = jax.nn.softmax(jnp.where(causal, scores, -jnp.inf), axis=-1).astype(jnp.bfloat16)
    context = jnp.einsum('bhqs,bshk->bqhk', attn_weights, values, preferred_element_type=jnp.float32).astype(jnp.bfloat16)
    attn_out = jnp.einsum('crd,de->cre', context.reshape(seq_count, seq_len, -1), w_out, preferred_element_type=jnp.float32)
    return (tokens.astype(jnp.float32) + attn_out).astype(jnp.bfloat16)


def router_gates(hidden, w_router, expert_ids):
    normed = rms_norm(hidden)
    logits = jnp.einsum('bsd,de->bse', normed, w_router, precision=lax.Precision.HIGHEST, preferred_element_type=jnp.float32)
    chosen = jnp.take_along_axis(logits, expert_ids, axis=-1)
    return normed.astype(jnp.bfloat16), jax.nn.softmax(chosen, axis=-1)


def dispatch_tables(ids_flat, experts, cap_rows):
    member = jnp.sum((ids_flat[:, :, None] == jnp.arange(experts, dtype=jnp.int32)).astype(jnp.int32), axis=1)
    before = jnp.cumsum(member, axis=0) - member
    slot = jnp.take_along_axis(before, ids_flat, axis=1)
    onehot = (member[:, :, None] > 0) & (before[:, :, None] == jnp.arange(cap_rows, dtype=jnp.int32))
    return onehot.astype(jnp.bfloat16), ids_flat * cap_rows + slot


def expert_ffn(rows, w_one, w_three, w_two):
    first = jnp.einsum('end,edf->enf', rows, w_one, preferred_element_type=jnp.float32)
    third = jnp.einsum('end,edf->enf', rows, w_three, preferred_element_type=jnp.float32)
    activated = (jax.nn.silu(first) * third).astype(jnp.bfloat16)
    return jnp.einsum('enf,efd->end', activated, w_two, preferred_element_type=jnp.float32).astype(jnp.bfloat16)


def combine_rows(hidden_flat, back_rows, flat_slot, gates_flat):
    table = back_rows.reshape(-1, back_rows.shape[-1])
    picked = jnp.take(table, flat_slot, axis=0)
    mixed = jnp.sum(gates_flat[:, :, None] * picked.astype(jnp.float32), axis=1)
    return (hidden_flat.astype(jnp.float32) + mixed).astype(jnp.bfloat16)


def solution(mesh):
    tok_spec = P(('dp', 'ep'))
    row_spec = P('ep')

    def local_layer(tokens, w_query, w_key, w_value, w_out, w_router, w_one, w_three, w_two, expert_ids):
        full_query = lax.all_gather(w_query, 'ep', axis=0, tiled=True)
        full_key = lax.all_gather(w_key, 'ep', axis=0, tiled=True)
        full_value = lax.all_gather(w_value, 'ep', axis=0, tiled=True)
        full_out = lax.all_gather(w_out, 'ep', axis=0, tiled=True)
        hidden = attention_layer(tokens, full_query, full_key, full_value, full_out)
        normed, gates = router_gates(hidden, w_router, expert_ids)
        seq_count, seq_len, model_dim = tokens.shape
        choices = expert_ids.shape[2]
        experts = w_router.shape[1]
        tok_count = seq_count * seq_len
        cap_rows = 2 * tok_count * choices // experts
        onehot, flat_slot = dispatch_tables(expert_ids.reshape(tok_count, choices), experts, cap_rows)
        send_rows = jnp.einsum('tec,td->ecd', onehot, normed.reshape(tok_count, model_dim), preferred_element_type=jnp.float32).astype(jnp.bfloat16)
        recv_rows = lax.all_to_all(send_rows, 'ep', 0, 1, tiled=True)
        done_rows = expert_ffn(recv_rows, w_one, w_three, w_two)
        back_rows = lax.all_to_all(done_rows, 'ep', 1, 0, tiled=True)
        layer_out = combine_rows(hidden.reshape(tok_count, model_dim), back_rows, flat_slot, gates.reshape(tok_count, choices))
        return layer_out.reshape(seq_count, seq_len, model_dim)

    return jax.shard_map(local_layer, mesh=mesh, in_specs=(tok_spec, row_spec, row_spec, row_spec, row_spec, P(), row_spec, row_spec, row_spec, tok_spec), out_specs=tok_spec, check_vma=False)
```

profile of v0, /device:TPU:81, one launch (start us, length us, event | category | flops | bytes accessed | tf_op | source)
XLA Modules:
  0.0 1185.6 jit_solution(7185515302224138909)
XLA Ops:
  6.6 0.7 all-gather.9.cloned.1.call-update
  7.4 0.7 all-gather.7.cloned.1.call-update
  8.2 0.7 all-gather.5.cloned.1.call-update
  9.0 0.6 all-gather.11.cloned.1.call-update
  9.6 0.1 copy.100
  9.7 1.6 convert_reduce_fusion
  11.4 0.1 copy.104
  11.5 0.1 fusion.57
  11.8 0.1 copy.103
  11.9 0.2 copy.108
  12.1 0.4 fusion.22
  12.6 83.1 %all-gather.9.cloned.1.call-done = bf16[2048,32,128]{2,1,0:T(8,128)(2,1)} async-done(((bf16[256,32,128]{2,1,0:T(8,128)(2,1)}), bf16[2048,32,128]{2,1,0:T(8,128)(2,1)}) %all-gather.9.cloned.1.call-update) | async-done | bytes 16777232 | tf_op jit(solution)/shard_map/all_gather | solution.py:65
  95.6 11.6 fusion.3
  107.2 72.6 %all-gather.7.cloned.1.call-done = bf16[2048,32,128]{2,1,0:T(8,128)(2,1)} async-done(((bf16[256,32,128]{2,1,0:T(8,128)(2,1)}), bf16[2048,32,128]{2,1,0:T(8,128)(2,1)}) %all-gather.7.cloned.1.call-update) | async-done | bytes 16777232 | tf_op jit(solution)/shard_map/all_gather | solution.py:64
  179.9 14.5 %fusion.31 = f32[3,32,128,128]{2,3,1,0:T(8,128)} fusion(bf16[3,128,32,128]{3,1,2,0:T(8,128)(2,1)} %fusion.3, bf16[2048,32,128]{2,1,0:T(8,128)(2,1)} %all-gather.7.cloned.1.call-done, bf16[3,128,2048]{2,1,0:T(8,128)(2,1)S(1)} %copy-done.5, f32[3,128]{1,0:T(4,128)S(1)} %add_rsqrt_fusion.1), kind=kOutput, calls=%fused_computation.47 | convolution fusion | flops 6849036288 | bytes 27788800 | tf_op jit(solution)/shard_map/bqhk,bshk->bhqs/dot_general | solution.py:22
  194.4 9.1 fusion.66
  203.5 60.6 %all-gather.5.cloned.1.call-done = bf16[2048,32,128]{2,1,0:T(8,128)(2,1)} async-done(((bf16[256,32,128]{2,1,0:T(8,128)(2,1)}), bf16[2048,32,128]{2,1,0:T(8,128)(2,1)}) %all-gather.5.cloned.1.call-update) | async-done | bytes 16777232 | tf_op jit(solution)/shard_map/all_gather | solution.py:66
  264.1 13.7 %fusion.38 = bf16[3,32,128,128]{3,2,1,0:T(8,128)(2,1)} fusion(f32[3,32,128,128]{2,3,1,0:T(8,128)} %get-tuple-element.6, f32[3,32,128]{2,1,0:T(8,128)S(1)} %get-tuple-element.5, bf16[2048,32,128]{2,1,0:T(8,128)(2,1)} %all-gather.5.cloned.1.call-done, bf16[3,128,2048]{2,1,0:T(8,128)(2,1)S(1)} %copy-done.5, f32[3,128]{1,0:T(4,128)S(1)} %add_rsqrt_fusion.1), kind=kOutput, calls=%fused_computation.52 | convolution fusion | flops 6853754880 | bytes 27837952 | tf_op jit(solution)/shard_map/bhqs,bshk->bqhk/dot_general | solution.py:25
  277.9 70.4 %all-gather.11.cloned.1.call-done = bf16[4096,2048]{1,0:T(8,128)(2,1)} async-done(((bf16[512,2048]{1,0:T(8,128)(2,1)}), bf16[4096,2048]{1,0:T(8,128)(2,1)}) %all-gather.11.cloned.1.call-update) | async-done | bytes 16777232 | tf_op jit(solution)/shard_map/all_gather | solution.py:67
  348.3 11.4 fusion.25
  359.7 1.1 copy-done.3
  360.8 0.3 fusion.20
  361.1 16.9 %convolution_convert_fusion.1 = bf16[128,48,2048]{2,0,1:T(8,128)(2,1)} fusion(bf16[384,2048,1]{1,0,2:T(8,128)(2,1)S(1)} %bitcast.114, s32[384,128]{0,1:T(8,128)S(1)} %bitcast_subtract_fusion, pred[384,128]{0,1:T(8,128)(4,1)S(1)} %copy.108), kind=kOutput, calls=%fused_computation.18 | convolution fusion | flops 9680977920 | bytes 26984448 | tf_op jit(solution)/shard_map/tec,td->ecd/dot_general | solution.py:76
  378.0 22.0 %copy.109 = bf16[128,48,2048]{2,1,0:T(8,128)(2,1)S(1)} copy(bf16[128,48,2048]{2,0,1:T(8,128)(2,1)} %convolution_convert_fusion.1) | data formatting | bytes 50331648 | tf_op jit(solution)/shard_map/convert_element_type | solution.py:76
  400.0 277.9 %all_to_all.33 = bf16[128,48,2048]{2,1,0:T(8,128)(2,1)} all-to-all(bf16[128,48,2048]{2,1,0:T(8,128)(2,1)S(1)} %copy.109), channel_id=1, replica_groups=mesh['dp'=4,'ep'=8] {'ep'}, dimensions={0} | all-to-all | bytes 50331648 | tf_op jit(solution)/shard_map/all_to_all | solution.py:77
  677.9 21.1 %copy.110 = bf16[8,16,48,2048]{3,2,0,1:T(8,128)(2,1)} copy(bf16[8,16,48,2048]{3,2,1,0:T(8,128)(2,1)} %bitcast.109) | data formatting | bytes 50331648 | tf_op jit(solution)/shard_map/all_to_all | solution.py:77
  699.0 35.6 %fusion.67 = f32[16,384,768]{2,1,0:T(8,128)} fusion(bf16[16,384,2048]{2,1,0:T(8,128)(2,1)} %bitcast.110, bf16[16,2048,768]{2,1,0:T(8,128)(2,1)} %param.16), kind=kOutput, calls=%fused_computation.88 | convolution fusion | flops 19327352832 | bytes 94371840 | tf_op jit(solution)/shard_map/end,edf->enf/dot_general | solution.py:46
  734.6 58.9 %convolution_convert_fusion = bf16[16,384,2048]{2,1,0:T(8,128)(2,1)} fusion(bf16[16,768,2048]{2,1,0:T(8,128)(2,1)} %param.18, f32[16,384,768]{2,1,0:T(8,128)} %fusion.67, bf16[16,384,2048]{2,1,0:T(8,128)(2,1)} %bitcast.111, bf16[16,2048,768]{2,1,0:T(8,128)(2,1)} %param.17), kind=kOutput, calls=%fused_computation.17 | convolution fusion | flops 38695600128 | bytes 169869312 | tf_op jit(solution)/shard_map/enf,efd->end/dot_general | solution.py:49
  793.5 26.8 %copy.111 = bf16[16,384,2048]{2,0,1:T(8,128)(2,1)} copy(bf16[16,384,2048]{2,1,0:T(8,128)(2,1)} %convolution_convert_fusion) | data formatting | bytes 50331648 | tf_op jit(solution)/shard_map/convert_element_type | solution.py:49
  820.3 7.9 all-to-all-start.1
  828.4 0.1 reshape.219
  828.5 0.6 copy-done.2
  829.1 24.9 %gather_fusion.2 = s32[3072]{0:T(1024)S(1)} fusion(s32[384,128]{0,1:T(8,128)S(1)} %copy-done.2, s32[3072]{0:T(1024)S(1)} %reshape.219), kind=kCustom, calls=%fused_computation.2 | custom fusion | bytes 49152 | tf_op jit(solution)/shard_map/jit(take_along_axis)/gather | solution.py:40
  854.1 0.1 gather.16
  854.2 0.1 reshape.222
  854.4 0.1 copy.114
  854.6 0.1 reshape.207
  854.9 0.1 reshape.213
  855.1 0.2 copy.107
  855.3 2.7 fusion.21
  858.0 25.0 %gather_fusion.1 = f32[3072]{0:T(1024)S(1)} fusion(f32[3,128,128]{2,1,0:T(8,128)S(1)} %fusion.21, s32[3072]{0:T(1024)S(1)} %reshape.213), kind=kCustom, calls=%fused_computation.1 | custom fusion | bytes 61440 | tf_op jit(solution)/shard_map/jit(take_along_axis)/gather | solution.py:33
  883.1 0.1 reshape.216
  883.4 0.1 copy.99
  883.5 217.9 %all-to-all-done.1 = bf16[16,384,2048]{2,0,1:T(8,128)(2,1)} async-done(((bf16[16,384,2048]{2,0,1:T(8,128)(2,1)}), bf16[16,384,2048]{2,0,1:T(8,128)(2,1)}, u32[]{:S(2)}, u32[]{:S(2)}) %all-to-all-start.1) | async-done | bytes 25165856 | tf_op jit(solution)/shard_map/all_to_all | solution.py:79
  1101.4 26.8 %copy.112 = bf16[16,8,48,2048]{3,2,0,1:T(8,128)(2,1)} copy(bf16[16,8,48,2048]{3,0,2,1:T(8,128)(2,1)} %bitcast.27) | data formatting | bytes 50331648 | tf_op jit(solution)/shard_map/all_to_all | solution.py:79
  1128.3 35.2 %gather_fusion = bf16[3072,2048]{1,0:T(8,128)(2,1)} fusion(bf16[6144,2048]{1,0:T(8,128)(2,1)} %bitcast.108, s32[3072]{0:T(1024)S(1)} %broadcast_clamp_fusion), kind=kCustom, calls=%fused_computation | custom fusion | bytes 25178112 | tf_op jit(solution)/shard_map/jit(_take)/gather | solution.py:54
  1163.5 13.4 %multiply_reduce_fusion = f32[384,2048]{1,0:T(8,128)S(1)} fusion(bf16[3072,2048]{1,0:T(8,128)(2,1)} %gather_fusion, f32[384,8]{1,0:T(8,128)S(1)} %copy.99, pred[384,8]{1,0:T(8,128)(4,1)S(1)} %copy.107), kind=kLoop, calls=%fused_computation.4 | loop fusion | flops 24379392 | bytes 15744000 | tf_op jit(solution)/shard_map/reduce_sum | solution.py:55
  1176.9 1.7 fusion.26
  (44 shorter events, 1.1 us)
Async XLA Ops:
  6.5 848.7 %copy-start = (f32[2048,128]{1,0:T(8,128)S(1)}, f32[2048,128]{1,0:T(8,128)}, u32[]{:S(2)}) copy-start(f32[2048,128]{1,0:T(8,128)} %param.15) | copy-start | bytes 3145732
  6.6 89.1 %all-gather.9.cloned.1.call-start = ((), (), s32[]{:S(2)}) async-start(), calls=%async_computation.4 | async-start | bytes 18874368 | tf_op jit(solution)/shard_map/all_gather | solution.py:65
  7.3 2.3 copy-start.6
  7.3 172.6 %all-gather.7.cloned.1.call-start = ((), (), s32[]{:S(2)}) async-start(), calls=%async_computation.3 | async-start | bytes 18874368 | tf_op jit(solution)/shard_map/all_gather | solution.py:64
  8.1 256.0 %all-gather.5.cloned.1.call-start = ((), (), s32[]{:S(2)}) async-start(), calls=%async_computation.2 | async-start | bytes 18874368 | tf_op jit(solution)/shard_map/all_gather | solution.py:66
  8.9 3.2 copy-start.5
  8.9 339.3 %all-gather.11.cloned.1.call-start = ((), (), s32[]{:S(2)}) async-start(), calls=%async_computation.5 | async-start | bytes 18874368 | tf_op jit(solution)/shard_map/all_gather | solution.py:67
  12.6 348.6 %copy-start.1 = (s32[384,128]{0,1:T(8,128)}, s32[384,128]{0,1:T(8,128)S(1)}, u32[]{:S(2)}) copy-start(s32[384,128]{0,1:T(8,128)S(1)} %bitcast_subtract_fusion) | copy-start | bytes 589828
  359.6 1.1 copy-start.3
  359.7 18.3 %copy-start.8 = (f32[3,128]{1,0:T(4,128)}, f32[3,128]{1,0:T(4,128)S(1)}, u32[]{:S(2)}) copy-start(f32[3,128]{1,0:T(4,128)S(1)} %add_rsqrt_fusion) | copy-start | bytes 4612
  820.3 7.9 copy-start.7
  820.3 281.1 %all-to-all-start.1 = ((bf16[16,384,2048]{2,0,1:T(8,128)(2,1)}), bf16[16,384,2048]{2,0,1:T(8,128)(2,1)}, u32[]{:S(2)}, u32[]{:S(2)}) async-start(bf16[16,384,2048]{2,0,1:T(8,128)(2,1)} %copy.111), calls=%async_computation.1 | async-start | bytes 50331648 | tf_op jit(solution)/shard_map/all_to_all | solution.py:79
  828.2 0.9 copy-start.2
  829.1 26.2 %copy-start.4 = (bf16[3,128,2048]{2,1,0:T(8,128)(2,1)S(1)}, bf16[3,128,2048]{2,1,0:T(8,128)(2,1)}, u32[]{:S(2)}) copy-start(bf16[3,128,2048]{2,1,0:T(8,128)(2,1)} %copy-done.3) | copy-start | bytes 4718596
  829.1 26.2 %copy-start.9 = (f32[3,128]{1,0:T(4,128)S(1)}, f32[3,128]{1,0:T(4,128)}, u32[]{:S(2)}) copy-start(f32[3,128]{1,0:T(4,128)} %copy-done.8) | copy-start | bytes 4612
Sparse Core Ops, SparseCore 0:
  9.0 86.6 all-gather.8
  97.2 82.5 all-gather.6
  181.5 82.5 all-gather.4
  265.6 82.5 all-gather.10
where the time goes:
time: 1200 us; the launch traced here: 1190 us
  waiting for transfers between devices  507 us (42%)
  blocking collectives  278 us (23%)
  local copies, waits for them, and re-layouts  186 us (16%)
  matrix products  165 us (14%)
  other arithmetic  27.1 us (2%)
  between operations  14 us (1%)
    all_to_all x1, blocking collectives, local_layer(): recv_rows = lax.all_to_all(send_rows, 'ep', 0, 1, tiled=True)  278 us
    all_to_all x1, waiting for transfers between devices, local_layer(): back_rows = lax.all_to_all(done_rows, 'ep', 1, 0, tiled=True)  218 us
    all_gather x1, waiting for transfers between devices, local_layer(): full_key = lax.all_gather(w_key, 'ep', axis=0, tiled=True)  83.1 us
    all_gather x1, waiting for transfers between devices, local_layer(): full_query = lax.all_gather(w_query, 'ep', axis=0, tiled=True)  72.6 us
    all_gather x1, waiting for transfers between devices, local_layer(): full_out = lax.all_gather(w_out, 'ep', axis=0, tiled=True)  70.4 us
    all_gather x1, waiting for transfers between devices, local_layer(): full_value = lax.all_gather(w_value, 'ep', axis=0, tiled=True)  60.6 us
    dot_general x1, matrix products, expert_ffn(): jnp.einsum('enf,efd->end', activated, w_two, preferred_element_type=jnp.f...  58.9 us
    dot_general x1, matrix products, expert_ffn(): jnp.einsum('end,edf->enf', rows, w_one, preferred_element_type=jnp.float32)  35.6 us
  transfers between devices with their start and end apart: 5, of which 5 were waited for; matrix products, arithmetic and copies ran while one was open for 9% of the time, Pallas kernels for 0%

commit v1 on v0

v1 whole, which is shorter than its diff:
```python
import functools

import jax
import jax.numpy as jnp
from jax import lax
from jax.experimental import pallas as pl
from jax.experimental.pallas import tpu as pltpu
from jax.sharding import PartitionSpec as P

EPS = 1e-6
SLOT = 16


def rms_norm(vals):
    wide = vals.astype(jnp.float32)
    return wide * lax.rsqrt(jnp.mean(wide * wide, axis=-1, keepdims=True) + EPS)


def attention_layer(tokens, w_query, w_key, w_value, w_out):
    seq_count = tokens.shape[0]
    seq_len = tokens.shape[1]
    head_dim = w_query.shape[2]
    normed = rms_norm(tokens).astype(jnp.bfloat16)
    query = jnp.einsum('bsd,dhk->bshk', normed, w_query, preferred_element_type=jnp.float32).astype(jnp.bfloat16)
    keys = jnp.einsum('bsd,dhk->bshk', normed, w_key, preferred_element_type=jnp.float32).astype(jnp.bfloat16)
    values = jnp.einsum('bsd,dhk->bshk', normed, w_value, preferred_element_type=jnp.float32).astype(jnp.bfloat16)
    scores = jnp.einsum('bqhk,bshk->bhqs', query, keys, preferred_element_type=jnp.float32) * head_dim ** -0.5
    causal = lax.broadcasted_iota(jnp.int32, (seq_len, seq_len), 0) >= lax.broadcasted_iota(jnp.int32, (seq_len, seq_len), 1)
    attn_weights = jax.nn.softmax(jnp.where(causal, scores, -jnp.inf), axis=-1).astype(jnp.bfloat16)
    context = jnp.einsum('bhqs,bshk->bqhk', attn_weights, values, preferred_element_type=jnp.float32).astype(jnp.bfloat16)
    attn_out = jnp.einsum('crd,de->cre', context.reshape(seq_count, seq_len, -1), w_out, preferred_element_type=jnp.float32)
    return (tokens.astype(jnp.float32) + attn_out).astype(jnp.bfloat16)


def slot_table(ids_flat, experts):
    tok_count = ids_flat.shape[0]
    member = jnp.any(ids_flat[:, :, None] == jnp.arange(experts, dtype=jnp.int32), axis=1)
    strict = lax.broadcasted_iota(jnp.int32, (tok_count, tok_count), 0) > lax.broadcasted_iota(jnp.int32, (tok_count, tok_count), 1)
    before = jnp.dot(strict.astype(jnp.bfloat16), member.astype(jnp.bfloat16), preferred_element_type=jnp.float32)
    return member, jnp.where(member, before.astype(jnp.int32), -1)


def dense_gates(hidden, w_router, member):
    normed = rms_norm(hidden)
    logits = jnp.dot(normed, w_router, precision=lax.Precision.HIGHEST, preferred_element_type=jnp.float32)
    top = jnp.max(jnp.where(member, logits, -jnp.inf), axis=1, keepdims=True)
    grown = jnp.where(member, jnp.exp(jnp.where(member, logits, top) - top), 0.0)
    return normed.astype(jnp.bfloat16), grown / jnp.sum(grown, axis=1, keepdims=True)


def dispatch_kernel(pos_ref, u_ref, out_ref, hot_ref):
    owned, toks = pos_ref.shape[1], pos_ref.shape[2]
    parts = out_ref.shape[1]
    cap = parts * SLOT
    lane = lax.broadcasted_iota(jnp.int32, (cap, toks), 0)
    for e in range(owned):
        hot_ref[e * cap:(e + 1) * cap, :] = jnp.where(lane == pos_ref[0, e:e + 1, :], 1.0, 0.0).astype(jnp.bfloat16)
    width = 512
    for c in range(u_ref.shape[1] // width):
        cols = slice(c * width, (c + 1) * width)
        rows = jnp.dot(hot_ref[...], u_ref[:, cols], preferred_element_type=jnp.float32).astype(jnp.bfloat16)
        out_ref[:, :, 0, :, cols] = rows.reshape(owned, parts, SLOT, width)


def dispatch(pos, u_all, parts):
    n, owned, toks = pos.shape
    dim = u_all.shape[1]
    return pl.pallas_call(
        dispatch_kernel,
        grid=(n,),
        in_specs=[pl.BlockSpec((1, owned, toks), lambda s: (s, 0, 0)), pl.BlockSpec((toks, dim), lambda s: (s, 0))],
        out_specs=pl.BlockSpec((owned, parts, 1, SLOT, dim), lambda s: (0, 0, s, 0, 0)),
        out_shape=jax.ShapeDtypeStruct((owned, parts, n, SLOT, dim), jnp.bfloat16),
        scratch_shapes=[pltpu.VMEM((owned * parts * SLOT, toks), jnp.bfloat16)],
        compiler_params=pltpu.CompilerParams(vmem_limit_bytes=60 * 2 ** 20),
        cost_estimate=pl.CostEstimate(flops=2 * n * owned * parts * SLOT * toks * dim, bytes_accessed=40_000_000, transcendentals=0),
        name="dispatch",
    )(pos, u_all)


def ffn_kernel(need_ref, rows_ref, one_ref, three_ref, two_ref, out_ref):
    parts, n = rows_ref.shape[1], rows_ref.shape[2]
    dim = rows_ref.shape[4]
    step = n * SLOT
    need = need_ref[pl.program_id(0)]
    for used in range(parts + 1):
        @pl.when(need == used)
        def _():
            if used:
                rows = rows_ref[0, :used].reshape(used * step, dim)
                first = jnp.dot(rows, one_ref[0], preferred_element_type=jnp.float32)
                third = jnp.dot(rows, three_ref[0], preferred_element_type=jnp.float32)
                acted = (jax.nn.silu(first) * third).astype(jnp.bfloat16)
                done = jnp.dot(acted, two_ref[0], preferred_element_type=jnp.float32).astype(jnp.bfloat16)
                out_ref[0, :used] = done.reshape(used, n, SLOT, dim)
            if used < parts:
                out_ref[0, used:] = jnp.zeros((parts - used, n, SLOT, dim), jnp.bfloat16)


def ffn(need, rows, w_one, w_three, w_two):
    owned, parts, n, _, dim = rows.shape
    inner = w_one.shape[2]
    tile = pl.BlockSpec((1, parts, n, SLOT, dim), lambda e, _: (e, 0, 0, 0, 0))
    return pl.pallas_call(
        ffn_kernel,
        grid_spec=pltpu.PrefetchScalarGridSpec(
            num_scalar_prefetch=1,
            grid=(owned,),
            in_specs=[
                tile,
                pl.BlockSpec((1, dim, inner), lambda e, _: (e, 0, 0)),
                pl.BlockSpec((1, dim, inner), lambda e, _: (e, 0, 0)),
                pl.BlockSpec((1, inner, dim), lambda e, _: (e, 0, 0)),
            ],
            out_specs=tile,
        ),
        out_shape=jax.ShapeDtypeStruct(rows.shape, jnp.bfloat16),
        compiler_params=pltpu.CompilerParams(vmem_limit_bytes=60 * 2 ** 20),
        cost_estimate=pl.CostEstimate(flops=6 * rows.size * inner, bytes_accessed=200_000_000, transcendentals=0),
        name="ffn",
    )(need, rows, w_one, w_three, w_two)


def combine_kernel(pos_ref, gate_ref, done_ref, out_ref, big_ref, mid_ref, low_ref):
    owned, toks = pos_ref.shape[1], pos_ref.shape[2]
    parts = done_ref.shape[1]
    cap = parts * SLOT
    lane = lax.broadcasted_iota(jnp.int32, (cap, toks), 0)
    gate = gate_ref[0]
    big = gate.astype(jnp.bfloat16).astype(jnp.float32)
    mid = (gate - big).astype(jnp.bfloat16).astype(jnp.float32)
    low = (gate - big) - mid
    for e in range(owned):
        here = lane == pos_ref[0, e:e + 1, :]
        rows = slice(e * cap, (e + 1) * cap)
        for ref, part in ((big_ref, big), (mid_ref, mid), (low_ref, low)):
            ref[rows, :] = jnp.where(here, part[e:e + 1, :], 0.0).astype(jnp.bfloat16)
    width = 512
    over = (((0,), (0,)), ((), ()))
    for c in range(out_ref.shape[1] // width):
        cols = slice(c * width, (c + 1) * width)
        done = done_ref[:, :, 0, :, cols].reshape(owned * cap, width)
        total = lax.dot_general(low_ref[...], done, over, preferred_element_type=jnp.float32)
        total += lax.dot_general(mid_ref[...], done, over, preferred_element_type=jnp.float32)
        out_ref[:, cols] = total + lax.dot_general(big_ref[...], done, over, preferred_element_type=jnp.float32)


def combine(pos, gates, done):
    n, owned, toks = pos.shape
    parts, dim = done.shape[1], done.shape[4]
    table = pl.BlockSpec((1, owned, toks), lambda s: (s, 0, 0))
    return pl.pallas_call(
        combine_kernel,
        grid=(n,),
        in_specs=[table, table, pl.BlockSpec((owned, parts, 1, SLOT, dim), lambda s: (0, 0, s, 0, 0))],
        out_specs=pl.BlockSpec((toks, dim), lambda s: (s, 0)),
        out_shape=jax.ShapeDtypeStruct((n * toks, dim), jnp.float32),
        scratch_shapes=[pltpu.VMEM((owned * parts * SLOT, toks), jnp.bfloat16)] * 3,
        compiler_params=pltpu.CompilerParams(vmem_limit_bytes=60 * 2 ** 20),
        cost_estimate=pl.CostEstimate(flops=6 * n * owned * parts * SLOT * toks * dim, bytes_accessed=60_000_000, transcendentals=0),
        name="combine",
    )(pos, gates, done)


def solution(mesh):
    tok_spec = P(('dp', 'ep'))
    row_spec = P('ep')
    groups = mesh.shape['dp']
    n = mesh.shape['ep']

    def gather_rows(weight):
        rows = weight.shape[0]
        if rows % (8 * groups):
            return lax.all_gather(weight, 'ep', axis=0, tiled=True)
        share = rows // groups
        piece = lax.dynamic_slice_in_dim(weight, lax.axis_index('dp') * share, share, 0)
        return lax.all_gather(piece, ('ep', 'dp'), axis=0, tiled=True)

    def local_layer(tokens, w_query, w_key, w_value, w_out, w_router, w_one, w_three, w_two, expert_ids):
        seq_count, seq_len, model_dim = tokens.shape
        choices = expert_ids.shape[2]
        experts = w_router.shape[1]
        owned = w_one.shape[0]
        toks = seq_count * seq_len
        parts = 2 * toks * choices // experts // SLOT

        member, slots = slot_table(expert_ids.reshape(toks, choices), experts)
        pos = lax.all_to_all(slots.T.reshape(n, owned, toks), 'ep', 0, 0, tiled=True)
        need = jnp.max(pos, axis=(0, 2)) // SLOT + 1

        full_query = gather_rows(w_query)
        full_key = gather_rows(w_key)
        full_value = gather_rows(w_value)
        full_out = gather_rows(w_out)
        hidden = attention_layer(tokens, full_query, full_key, full_value, full_out).reshape(toks, model_dim)
        normed, gates_local = dense_gates(hidden, w_router, member)
        u_all = lax.all_gather(normed, 'ep', axis=0, tiled=True)
        gates = lax.all_to_all(gates_local.T.reshape(n, owned, toks), 'ep', 0, 0, tiled=True)
        rows = dispatch(pos, u_all, parts)
        done = ffn(need, rows, w_one, w_three, w_two)
        partial = combine(pos, gates, done)
        mixed = lax.psum_scatter(partial, 'ep', scatter_dimension=0, tiled=True)
        layer_out = (hidden.astype(jnp.float32) + mixed).astype(jnp.bfloat16)
        return layer_out.reshape(seq_count, seq_len, model_dim)

    return jax.shard_map(local_layer, mesh=mesh, in_specs=(tok_spec, row_spec, row_spec, row_spec, row_spec, P(), row_spec, row_spec, row_spec, tok_spec), out_specs=tok_spec, check_vma=False)
```

time: 1200 us -> 787 us (0.66); the launches traced: 1190 us -> 786 us
  blocking collectives: 278 us -> 9.49 us
  local copies, waits for them, and re-layouts: 186 us -> 10.2 us
  Pallas kernels: 0 us -> 125 us
  matrix products: 165 us -> 55.4 us
  waiting for transfers between devices: 507 us -> 548 us
    all_to_all x1, blocking collectives: 278 us -> 9.49 us  [local_layer(): lax.all_to_all(slots.T.reshape(n, owned, toks), 'ep', 0, 0, tiled=True)]
    all_to_all x1, waiting for transfers between devices: 218 us -> 0.01 us  [local_layer(): lax.all_to_all(gates_local.T.reshape(n, owned, toks), 'ep', 0, 0, tiled=T...]
    reduce_scatter x0 -> x1, waiting for transfers between devices: none -> 131 us  [local_layer(): mixed = lax.psum_scatter(partial, 'ep', scatter_dimension=0, tiled=True)]
    all_gather x4 -> x5, waiting for transfers between devices: 287 us -> 417 us  [the longest x4 373 us: gather_rows(): return lax.all_gather(piece, ('ep', 'dp'), axis=0, tiled=True)]
    pallas_call x0 -> x3, Pallas kernels: none -> 125 us  [the longest x1 69.4 us: ffn(): pl.pallas_call(ffn_kernel, grid_spec=pltpu.PrefetchScalarGridSpec(num_sca...]
    dot_general x4 -> x2, matrix products: 114 us -> 4.51 us  [the longest x1 4.24 us: dense_gates(): jnp.dot(normed, w_router, precision=lax.Precision.HIGHEST, preferred_elem...]
    gather x13 -> x0, local copies, waits for them, and re-layouts: 86.3 us -> none  [the longest x1 35.2 us: combine_rows(): picked = jnp.take(table, flat_slot, axis=0)]
    convert_element_type x2 -> x0, local copies, waits for them, and re-layouts: 48.8 us -> none  [the longest x1 26.8 us: expert_ffn(): jnp.einsum('enf,efd->end', activated, w_two, preferred_element_type=jnp.f...]
  transfers between devices with their start and end apart: 5 -> 7, of which waited for: 5 -> 6; matrix products, arithmetic and copies ran while one was open for 9% -> 8% of each run, Pallas kernels for 0% -> 11%
where the time goes in v1:
time: 787 us; the launch traced here: 786 us
  waiting for transfers between devices  548 us (70%)
  Pallas kernels  125 us (16%)
  matrix products  55.4 us (7%)
  other arithmetic  18.7 us (2%)
  between operations  13.6 us (2%)
  local copies, waits for them, and re-layouts  10.2 us (1%)
  blocking collectives  9.49 us (1%)
    all_gather x4, waiting for transfers between devices, gather_rows(): return lax.all_gather(piece, ('ep', 'dp'), axis=0, tiled=True)  373 us
    reduce_scatter x1, waiting for transfers between devices, local_layer(): mixed = lax.psum_scatter(partial, 'ep', scatter_dimension=0, tiled=True)  131 us
    pallas_call x1, Pallas kernels, ffn(): pl.pallas_call(ffn_kernel, grid_spec=pltpu.PrefetchScalarGridSpec(num_sca...  69.4 us
    all_gather x1, waiting for transfers between devices, local_layer(): u_all = lax.all_gather(normed, 'ep', axis=0, tiled=True)  43.5 us
    pallas_call x1, Pallas kernels, combine(): pl.pallas_call(combine_kernel, grid=(n,), in_specs=[table, table, pl.Bloc...  35.8 us
    pallas_call x1, Pallas kernels, dispatch(): pl.pallas_call(dispatch_kernel, grid=(n,), in_specs=[pl.BlockSpec((1, own...  20.3 us
  transfers between devices with their start and end apart: 7, of which 6 were waited for; matrix products, arithmetic and copies ran while one was open for 8% of the time, Pallas kernels for 11%

profile of v1, /device:TPU:81, one launch (start us, length us, event | category | flops | bytes accessed | tf_op | source)
XLA Modules:
  0.0 785.7 jit_solution(157255446732634420)
XLA Ops:
  6.6 0.0 all-gather.10.cloned.1.call-start
  6.6 1.6 copy-done
  8.1 0.8 constant_dynamic-slice_fusion.1
  9.0 0.1 all-gather.10.cloned.1.call-update
  9.0 0.1 all-gather.8.cloned.1.call-start
  9.1 2.0 constant_dynamic-slice_fusion.2
  11.1 0.1 all-gather.8.cloned.1.call-update
  11.1 0.1 all-gather.6.cloned.1.call-start
  11.2 1.9 constant_dynamic-slice_fusion.3
  13.1 0.1 all-gather.6.cloned.1.call-update
  13.2 0.1 all-gather.12.cloned.1.call-start
  13.2 1.9 constant_dynamic-slice_fusion
  15.1 0.1 all-gather.12.cloned.1.call-update
  15.2 0.1 all-gather.14.cloned.1.call-start
  15.3 0.4 fusion.13
  15.7 103.7 %all-gather.10.cloned.1.call-done = bf16[2048,32,128]{2,1,0:T(8,128)(2,1)} async-done(((bf16[64,32,128]{2,1,0:T(8,128)(2,1)}), bf16[2048,32,128]{2,1,0:T(8,128)(2,1)}) %all-gather.10.cloned.1.call-update) | async-done | bytes 16777232 | tf_op jit(solution)/shard_map/all_gather | solution.py:177
  119.4 11.6 %fusion.3 = bf16[3,128,32,128]{3,1,2,0:T(8,128)(2,1)} fusion(bf16[2048,32,128]{2,1,0:T(8,128)(2,1)} %all-gather.10.cloned.1.call-done, bf16[3,128,2048]{2,1,0:T(8,128)(2,1)S(1)} %copy-done.4, f32[3,128]{1,0:T(4,128)S(1)} %add_rsqrt_fusion), kind=kOutput, calls=%fused_computation.3 | convolution fusion | flops 6444810240 | bytes 21497344 | tf_op jit(solution)/shard_map/bsd,dhk->bshk/dot_general | solution.py:25
  130.9 94.5 %all-gather.8.cloned.1.call-done = bf16[2048,32,128]{2,1,0:T(8,128)(2,1)} async-done(((bf16[64,32,128]{2,1,0:T(8,128)(2,1)}), bf16[2048,32,128]{2,1,0:T(8,128)(2,1)}) %all-gather.8.cloned.1.call-update) | async-done | bytes 16777232 | tf_op jit(solution)/shard_map/all_gather | solution.py:177
  225.4 14.5 %fusion.22 = f32[3,32,128,128]{2,3,1,0:T(8,128)} fusion(bf16[3,128,32,128]{3,1,2,0:T(8,128)(2,1)} %fusion.3, bf16[2048,32,128]{2,1,0:T(8,128)(2,1)} %all-gather.8.cloned.1.call-done, bf16[3,128,2048]{2,1,0:T(8,128)(2,1)S(1)} %copy-done.4, f32[3,128]{1,0:T(4,128)S(1)} %add_rsqrt_fusion), kind=kOutput, calls=%fused_computation.31 | convolution fusion | flops 6849036288 | bytes 27788800 | tf_op jit(solution)/shard_map/bqhk,bshk->bhqs/dot_general | solution.py:27
  239.9 9.1 %fusion.57 = (f32[3,32,128]{2,1,0:T(8,128)S(1)}, f32[3,32,128,128]{2,3,1,0:T(8,128)}) fusion(f32[3,32,128,128]{2,3,1,0:T(8,128)} %fusion.22, pred[128,128]{0,1:T(8,128)(4,1)S(1)} %iota_compare_fusion.3), kind=kOutput, calls=%fused_computation.66 | output fusion | flops 9437311 | bytes 12648448 | tf_op jit(solution)/shard_map/sub | solution.py:29
  249.1 82.4 %all-gather.6.cloned.1.call-done = bf16[2048,32,128]{2,1,0:T(8,128)(2,1)} async-done(((bf16[64,32,128]{2,1,0:T(8,128)(2,1)}), bf16[2048,32,128]{2,1,0:T(8,128)(2,1)}) %all-gather.6.cloned.1.call-update) | async-done | bytes 16777232 | tf_op jit(solution)/shard_map/all_gather | solution.py:177
  331.5 13.4 %fusion.29 = bf16[3,32,128,128]{3,2,1,0:T(8,128)(2,1)} fusion(f32[3,32,128,128]{2,3,1,0:T(8,128)} %get-tuple-element.8, f32[3,32,128]{2,1,0:T(8,128)S(1)} %get-tuple-element.7, bf16[2048,32,128]{2,1,0:T(8,128)(2,1)} %all-gather.6.cloned.1.call-done, bf16[3,128,2048]{2,1,0:T(8,128)(2,1)S(1)} %copy-done.4, f32[3,128]{1,0:T(4,128)S(1)} %add_rsqrt_fusion), kind=kOutput, calls=%fused_computation.36 | convolution fusion | flops 6853754880 | bytes 27837952 | tf_op jit(solution)/shard_map/bhqs,bshk->bqhk/dot_general | solution.py:30
  344.9 92.5 %all-gather.12.cloned.1.call-done = bf16[4096,2048]{1,0:T(8,128)(2,1)} async-done(((bf16[128,2048]{1,0:T(8,128)(2,1)}), bf16[4096,2048]{1,0:T(8,128)(2,1)}) %all-gather.12.cloned.1.call-update) | async-done | bytes 16777232 | tf_op jit(solution)/shard_map/all_gather | solution.py:177
  437.4 11.4 %fusion.17 = (f32[3,128]{1,0:T(4,128)S(1)}, bf16[3,128,2048]{2,1,0:T(8,128)(2,1)S(1)}) fusion(bf16[3,128,4096]{1,2,0:T(8,128)(2,1)} %bitcast.68, bf16[4096,2048]{1,0:T(8,128)(2,1)} %all-gather.12.cloned.1.call-done, bf16[3,128,2048]{2,1,0:T(8,128)(2,1)S(1)} %copy-done.4), kind=kOutput, calls=%fused_computation.26 | convolution fusion | flops 6447169024 | bytes 23070208 | tf_op jit(solution)/shard_map/crd,de->cre/dot_general | solution.py:31
  448.9 1.1 copy-done.2
  450.0 1.5 fusion.56
  451.5 0.1 all-gather.14.cloned.1.call-update
  451.6 0.1 copy.29
  451.7 2.0 fusion.33
  453.7 0.1 copy.30
  453.9 0.3 fusion.38
  454.2 9.5 %all_to_all.10.pos_ref = s32[8,16,384]{2,1,0:T(8,128)S(1)} all-to-all(s32[8,16,384]{2,1,0:T(8,128)S(1)} %bitcast.66), channel_id=1, replica_groups=mesh['dp'=4,'ep'=8] {'ep'}, dimensions={0} | all-to-all | bytes 393216 | tf_op jit(solution)/shard_map/all_to_all | solution.py:188
  463.7 0.1 reduce_max.29
  463.8 0.6 fusion.53.need_ref
  464.4 4.2 select_reduce_fusion.1
  468.6 0.1 select_reduce_fusion
  468.7 0.7 fusion.51
  469.5 4.8 all-to-all-start.1
  474.3 43.5 %all-gather.14.cloned.1.call-done.u_ref = bf16[3072,2048]{1,0:T(8,128)(2,1)} async-done(((bf16[384,2048]{1,0:T(8,128)(2,1)}), bf16[3072,2048]{1,0:T(8,128)(2,1)}) %all-gather.14.cloned.1.call-update) | async-done | bytes 12582928 | tf_op jit(solution)/shard_map/all_gather | solution.py:197
  517.7 20.3 %dispatch.1.rows_ref = bf16[16,3,8,16,2048]{4,3,2,1,0:T(8,128)(2,1)} custom-call(s32[8,16,384]{2,1,0:T(8,128)} %copy-done.3, bf16[3072,2048]{1,0:T(8,128)(2,1)} %all-gather.14.cloned.1.call-done.u_ref), custom_call_target="tpu_custom_call" | custom-call | flops 9663676416 | bytes 40000000 | tf_op jit(solution)/shard_map/dispatch/pallas_call | solution.py:68
  538.0 69.4 %ffn.1.done_ref = bf16[16,3,8,16,2048]{4,3,2,1,0:T(8,128)(2,1)} custom-call(s32[16]{0:T(128)} %fusion.53.need_ref, bf16[16,3,8,16,2048]{4,3,2,1,0:T(8,128)(2,1)} %dispatch.1.rows_ref, bf16[16,2048,768]{2,1,0:T(8,128)(2,1)} %one_ref.1, bf16[16,2048,768]{2,1,0:T(8,128)(2,1)} %three_ref.1, bf16[16,768,2048]{2,1,0:T(8,128)(2,1)} %two_ref.1), custom_call_target="tpu_custom_call" | custom-call | flops 57982058496 | bytes 200000000 | tf_op jit(solution)/shard_map/ffn/pallas_call | solution.py:104
  607.4 0.0 all-to-all-done.1.gate_ref
  607.4 0.7 copy-done.5
  608.1 35.8 %combine.1 = f32[3072,2048]{1,0:T(8,128)} custom-call(s32[8,16,384]{2,1,0:T(8,128)} %copy-done.3, f32[8,16,384]{2,1,0:T(8,128)} %copy-done.5, bf16[16,3,8,16,2048]{4,3,2,1,0:T(8,128)(2,1)} %ffn.1.done_ref), custom_call_target="tpu_custom_call" | custom-call | flops 28991029248 | bytes 60000000 | tf_op jit(solution)/shard_map/combine/pallas_call | solution.py:152
  643.9 0.1 reduce-scatter.2.cloned.1.call-update
  644.0 0.0 copy-start.1
  644.0 130.9 %reduce-scatter.2.cloned.1.call-done = f32[384,2048]{1,0:T(8,128)} async-done(((f32[3072,2048]{1,0:T(8,128)}), f32[384,2048]{1,0:T(8,128)}) %reduce-scatter.2.cloned.1.call-update) | async-done | bytes 3145744 | tf_op jit(solution)/shard_map/reduce_scatter | solution.py:202
  774.8 4.0 fusion.18
  (14 shorter events, 0.1 us)
Async XLA Ops:
  6.5 1.6 copy-start
  6.6 112.8 %all-gather.10.cloned.1.call-start = ((), (), s32[]{:S(2)}) async-start(), calls=%async_computation.5 | async-start | bytes 17301504 | tf_op jit(solution)/shard_map/all_gather | solution.py:177
  9.0 6.3 copy-start.4
  9.0 216.4 %all-gather.8.cloned.1.call-start = ((), (), s32[]{:S(2)}) async-start(), calls=%async_computation.4 | async-start | bytes 17301504 | tf_op jit(solution)/shard_map/all_gather | solution.py:177
  11.1 320.4 %all-gather.6.cloned.1.call-start = ((), (), s32[]{:S(2)}) async-start(), calls=%async_computation.3 | async-start | bytes 17301504 | tf_op jit(solution)/shard_map/all_gather | solution.py:177
  13.2 424.3 %all-gather.12.cloned.1.call-start = ((), (), s32[]{:S(2)}) async-start(), calls=%async_computation.6 | async-start | bytes 17301504 | tf_op jit(solution)/shard_map/all_gather | solution.py:177
  15.2 502.6 %all-gather.14.cloned.1.call-start = ((), (), s32[]{:S(2)}) async-start(), calls=%async_computation.7 | async-start | bytes 14155776 | tf_op jit(solution)/shard_map/all_gather | solution.py:197
  448.8 1.1 copy-start.2
  450.0 1.6 copy-start.6
  463.7 54.1 %copy-start.3 = (s32[8,16,384]{2,1,0:T(8,128)}, s32[8,16,384]{2,1,0:T(8,128)S(1)}, u32[]{:S(2)}) copy-start(s32[8,16,384]{2,1,0:T(8,128)S(1)} %all_to_all.10.pos_ref) | copy-start | bytes 589828
  469.5 138.0 %all-to-all-start.1 = ((f32[8,16,384]{2,1,0:T(8,128)}), f32[8,16,384]{2,1,0:T(8,128)S(1)}, u32[]{:S(2)}, u32[]{:S(2)}) async-start(f32[8,16,384]{2,1,0:T(8,128)} %bitcast.15), calls=%async_computation.1 | async-start | bytes 393216 | tf_op jit(solution)/shard_map/all_to_all | solution.py:198
  474.2 300.6 %reduce-scatter.2.cloned.1.call-start = ((), (), s32[]{:S(2)}) async-start(), calls=%async_computation.8 | async-start | bytes 28311552 | tf_op jit(solution)/shard_map/reduce_scatter | solution.py:202
  607.4 0.7 copy-start.5
  644.0 134.9 %copy-start.1 = (bf16[256,32,128]{2,1,0:T(8,128)(2,1)S(1)}, bf16[256,32,128]{2,1,0:T(8,128)(2,1)}, u32[]{:S(2)}) copy-start(bf16[256,32,128]{2,1,0:T(8,128)(2,1)} %param.12) | copy-start | bytes 6291460
Sparse Core Ops, SparseCore 0:
  10.2 109.0 all-gather.9
  122.3 103.1 all-gather.7
  228.3 103.1 all-gather.5
  334.3 103.1 all-gather.11
  451.7 66.0 all-gather.13
  644.1 130.7 reduce-scatter.1

commit v2 on v1

--- a/solution.py
+++ b/solution.py
@@ -9,6 +9,7 @@
 
 EPS = 1e-6
 SLOT = 16
+MESH = pl.DeviceIdType.MESH
 
 
 def rms_norm(vals):
@@ -16,20 +17,213 @@
     return wide * lax.rsqrt(jnp.mean(wide * wide, axis=-1, keepdims=True) + EPS)
 
 
-def attention_layer(tokens, w_query, w_key, w_value, w_out):
-    seq_count = tokens.shape[0]
-    seq_len = tokens.shape[1]
-    head_dim = w_query.shape[2]
-    normed = rms_norm(tokens).astype(jnp.bfloat16)
-    query = jnp.einsum('bsd,dhk->bshk', normed, w_query, preferred_element_type=jnp.float32).astype(jnp.bfloat16)
-    keys = jnp.einsum('bsd,dhk->bshk', normed, w_key, preferred_element_type=jnp.float32).astype(jnp.bfloat16)
-    values = jnp.einsum('bsd,dhk->bshk', normed, w_value, preferred_element_type=jnp.float32).astype(jnp.bfloat16)
-    scores = jnp.einsum('bqhk,bshk->bhqs', query, keys, preferred_element_type=jnp.float32) * head_dim ** -0.5
+def attend_kernel(mesh_n, seq_len, x_ref, wq_ref, wk_ref, wv_ref, wo_ref, h_ref, fq_ref, fk_ref, fv_ref, fo_ref,
+                  n_ref, q_ref, k_ref, v_ref, wide_ref, tall_ref, send, recv, load_sem):
+    me = lax.axis_index('ep')
+    dp = lax.axis_index('dp')
+    core = me % 2
+    odd = dp % 2
+    right = (me + 2) % mesh_n
+    left = (me + mesh_n - 2) % mesh_n
+    across = (me + mesh_n // 2) % mesh_n
+    sibling = me + 1 - 2 * core
+    partner = dp + 1 - 2 * odd
+    own_refs = (wq_ref, wk_ref, wv_ref, wo_ref)
+    full_refs = (fq_ref, fk_ref, fv_ref, fo_ref)
+
+    barrier = pltpu.get_barrier_semaphore()
+    for peer in (right, left, sibling):
+        pl.semaphore_signal(barrier, inc=1, device_id={'ep': peer}, device_id_type=MESH)
+    pl.semaphore_signal(barrier, inc=1, device_id={'dp': partner}, device_id_type=MESH)
+    pl.semaphore_wait(barrier, 4)
+
+    def spans(m):
+        unit = own_refs[m].shape[0] // 16
+        def at(even_off, odd_off, size):
+            return pl.ds(pl.multiple_of((even_off + odd * (odd_off - even_off)) * unit, unit), size * unit)
+        return {'F': at(0, 10, 6), 'S': at(6, 5, 5), 'X': at(0, 5, 11), 'ZS': at(0, 11, 5), 'ZR': at(11, 0, 5)}
+
+    def ways(m):
+        return (right, left) if m % 2 == 0 else (left, right)
+
+    def copy(m, slot, src, dst, peer):
+        return pltpu.make_async_remote_copy(src_ref=src, dst_ref=dst, send_sem=send.at[m, slot], recv_sem=recv.at[m, slot],
+                                            device_id=peer, device_id_type=MESH)
+
+    def outgoing(m, slot):
+        full, own, span, (fore, back) = full_refs[m], own_refs[m], spans(m), ways(m)
+        if slot < 4:
+            rows = span['FSSF'[slot]]
+            return copy(m, slot, own.at[rows], full.at[me, rows], {'ep': fore if slot < 2 else back})
+        if slot < 6:
+            rows, source = (span['F'], back) if slot == 4 else (span['S'], fore)
+            return copy(m, slot, full.at[source, rows], full.at[source, rows], {'ep': fore if slot == 4 else back})
+        if slot < 9:
+            source, rows = (back, fore, across)[slot - 6], span['ZS']
+            return copy(m, slot, full.at[source, rows], full.at[source, rows], {'dp': partner})
+        if slot == 9:
+            return copy(m, slot, own, full.at[me], {'ep': sibling})
+        source, rows = (back, fore, across)[(slot - 10) % 3], span['X' if slot < 13 else 'ZR']
+        return copy(m, slot, full.at[source, rows], full.at[source, rows], {'ep': sibling})
+
+    def arrived(m, slot):
+        full, span, (fore, back) = full_refs[m], spans(m), ways(m)
+        if slot < 4:
+            dst = full.at[back if slot < 2 else fore, span['FSSF'[slot]]]
+        elif slot < 6:
+            dst = full.at[across, span['F' if slot == 4 else 'S']]
+        elif slot < 9:
+            dst = full.at[(back, fore, across)[slot - 6], span['ZR']]
+        elif slot == 9:
+            dst = full.at[sibling]
+        else:
+            source = (back, fore, across)[(slot - 10) % 3]
+            dst = full.at[source + 1 - 2 * core, span['X' if slot < 13 else 'ZR']]
+        copy(m, slot, dst, dst, {'ep': sibling}).wait_recv()
+
+    def start(m, *slots):
+        for slot in slots:
+            outgoing(m, slot).start()
+
+    def own(m):
+        start(m, 0, 2, 1, 3, 9)
+
+    def near(m):
+        arrived(m, 0)
+        start(m, 4, 6)
+        arrived(m, 2)
+        start(m, 5)
+        arrived(m, 1)
+        start(m, 10)
+        arrived(m, 3)
+        start(m, 7, 11)
+
+    def far(m):
+        arrived(m, 4)
+        start(m, 8)
+        arrived(m, 5)
+        start(m, 12)
+
+    def zside(m):
+        for slot in (6, 7, 8):
+            arrived(m, slot)
+            start(m, slot + 7)
+
+    def finish(m):
+        for slot in range(9, 16):
+            arrived(m, slot)
+
+    def stream(m, buf, width, body):
+        full, mine = full_refs[m], own_refs[m]
+        total = full.shape[2] // width
+        def cols(c):
+            return pl.ds(pl.multiple_of(c * width, width), width)
+        def fetch(c, slot):
+            pltpu.make_async_copy(mine.at[:, cols(c)], buf.at[slot, me], load_sem.at[slot]).start()
+            for j in range(1, mesh_n):
+                owner = (me + j) % mesh_n
+                pltpu.make_async_copy(full.at[owner, :, cols(c)], buf.at[slot, owner], load_sem.at[slot]).start()
+        fetch(0, 0)
+        def step(c, carry):
+            slot = c % 2
+            @pl.when(c + 1 < total)
+            def _():
+                fetch(c + 1, 1 - slot)
+            pltpu.make_async_copy(full.at[:, :, cols(c)], buf.at[slot], load_sem.at[slot]).wait()
+            body(cols(c), buf[slot].reshape(full.shape[0] * full.shape[1], width))
+            return carry
+        lax.fori_loop(0, total, step, 0)
+
+    def project(m, out):
+        def body(cols, chunk):
+            out[:, cols] = jnp.dot(n_ref[...], chunk, preferred_element_type=jnp.float32).astype(jnp.bfloat16)
+        stream(m, wide_ref, wide_ref.shape[3], body)
+
+    head_dim = 128
+    seqs = x_ref.shape[0] // seq_len
     causal = lax.broadcasted_iota(jnp.int32, (seq_len, seq_len), 0) >= lax.broadcasted_iota(jnp.int32, (seq_len, seq_len), 1)
-    attn_weights = jax.nn.softmax(jnp.where(causal, scores, -jnp.inf), axis=-1).astype(jnp.bfloat16)
-    context = jnp.einsum('bhqs,bshk->bqhk', attn_weights, values, preferred_element_type=jnp.float32).astype(jnp.bfloat16)
-    attn_out = jnp.einsum('crd,de->cre', context.reshape(seq_count, seq_len, -1), w_out, preferred_element_type=jnp.float32)
-    return (tokens.astype(jnp.float32) + attn_out).astype(jnp.bfloat16)
+
+    def attention(first, last):
+        def step(i, carry):
+            for b in range(seqs):
+                rows = slice(b * seq_len, (b + 1) * seq_len)
+                for j in range(2):
+                    cols = pl.ds(pl.multiple_of((2 * i + j) * head_dim, head_dim), head_dim)
+                    scores = lax.dot_general(q_ref[rows, cols], k_ref[rows, cols], (((1,), (1,)), ((), ())),
+                                             preferred_element_type=jnp.float32) * head_dim ** -0.5
+                    scores = jnp.where(causal, scores, -jnp.inf)
+                    grown = jnp.exp(scores - jnp.max(scores, axis=1, keepdims=True))
+                    weights = (grown * (1.0 / jnp.sum(grown, axis=1, keepdims=True))).astype(jnp.bfloat16)
+                    q_ref[rows, cols] = jnp.dot(weights, v_ref[rows, cols], preferred_element_type=jnp.float32).astype(jnp.bfloat16)
+            return carry
+        lax.fori_loop(first, last, step, 0)
+
+    own(0)
+    own(1)
+    wide = x_ref[...].astype(jnp.float32)
+    n_ref[...] = (wide * lax.rsqrt(jnp.mean(wide * wide, axis=-1, keepdims=True) + EPS)).astype(jnp.bfloat16)
+    near(0)
+    own(2)
+    near(1)
+    far(0)
+    zside(0)
+    finish(0)
+    project(0, q_ref)
+    near(2)
+    far(1)
+    zside(1)
+    finish(1)
+    own(3)
+    project(1, k_ref)
+    far(2)
+    zside(2)
+    finish(2)
+    project(2, v_ref)
+    pairs = q_ref.shape[1] // head_dim // 2
+    attention(0, pairs // 2)
+    near(3)
+    attention(pairs // 2, pairs)
+    far(3)
+    zside(3)
+    finish(3)
+
+    def out_body(cols, chunk):
+        mixed = jnp.dot(q_ref[...], chunk, preferred_element_type=jnp.float32)
+        h_ref[:, cols] = (x_ref[:, cols].astype(jnp.float32) + mixed).astype(jnp.bfloat16)
+    stream(3, tall_ref, tall_ref.shape[3], out_body)
+    for m in range(4):
+        for slot in range(16):
+            outgoing(m, slot).wait_send()
+
+
+def attend(mesh_n, seq_len, x, wq, wk, wv, wo):
+    toks, dim = x.shape
+    width = wq.shape[1]
+    bf = jnp.bfloat16
+    vmem = pl.BlockSpec(memory_space=pltpu.VMEM)
+    hbm = pl.BlockSpec(memory_space=pltpu.HBM)
+    fulls = [jax.ShapeDtypeStruct((mesh_n,) + w.shape, bf) for w in (wq, wk, wv, wo)]
+    out = pl.pallas_call(
+        functools.partial(attend_kernel, mesh_n, seq_len),
+        in_specs=[vmem, hbm, hbm, hbm, hbm],
+        out_specs=[vmem, hbm, hbm, hbm, hbm],
+        out_shape=[jax.ShapeDtypeStruct((toks, dim), bf)] + fulls,
+        scratch_shapes=[
+            pltpu.VMEM((toks, dim), bf),
+            pltpu.VMEM((toks, width), bf),
+            pltpu.VMEM((toks, width), bf),
+            pltpu.VMEM((toks, width), bf),
+            pltpu.VMEM((2, mesh_n, wq.shape[0], min(512, width)), bf),
+            pltpu.VMEM((2, mesh_n, wo.shape[0], min(256, dim)), bf),
+            pltpu.SemaphoreType.DMA((4, 16)),
+            pltpu.SemaphoreType.DMA((4, 16)),
+            pltpu.SemaphoreType.DMA((2,)),
+        ],
+        compiler_params=pltpu.CompilerParams(collective_id=0, has_side_effects=True, vmem_limit_bytes=56 * 2 ** 20),
+        cost_estimate=pl.CostEstimate(flops=8 * toks * dim * width, bytes_accessed=200_000_000, transcendentals=0),
+        name='attend',
+    )(x, wq, wk, wv, wo)
+    return out[0]
 
 
 def slot_table(ids_flat, experts):
@@ -165,16 +359,7 @@
 def solution(mesh):
     tok_spec = P(('dp', 'ep'))
     row_spec = P('ep')
-    groups = mesh.shape['dp']
     n = mesh.shape['ep']
-
-    def gather_rows(weight):
-        rows = weight.shape[0]
-        if rows % (8 * groups):
-            return lax.all_gather(weight, 'ep', axis=0, tiled=True)
-        share = rows // groups
-        piece = lax.dynamic_slice_in_dim(weight, lax.axis_index('dp') * share, share, 0)
-        return lax.all_gather(piece, ('ep', 'dp'), axis=0, tiled=True)
 
     def local_layer(tokens, w_query, w_key, w_value, w_out, w_router, w_one, w_three, w_two, expert_ids):
         seq_count, seq_len, model_dim = tokens.shape
@@ -188,11 +373,8 @@
         pos = lax.all_to_all(slots.T.reshape(n, owned, toks), 'ep', 0, 0, tiled=True)
         need = jnp.max(pos, axis=(0, 2)) // SLOT + 1
 
-        full_query = gather_rows(w_query)
-        full_key = gather_rows(w_key)
-        full_value = gather_rows(w_value)
-        full_out = gather_rows(w_out)
-        hidden = attention_layer(tokens, full_query, full_key, full_value, full_out).reshape(toks, model_dim)
+        flat = [w.reshape(w.shape[0], -1) for w in (w_query, w_key, w_value, w_out)]
+        hidden = attend(n, seq_len, tokens.reshape(toks, model_dim), *flat)
         normed, gates_local = dense_gates(hidden, w_router, member)
         u_all = lax.all_gather(normed, 'ep', axis=0, tiled=True)
         gates = lax.all_to_all(gates_local.T.reshape(n, owned, toks), 'ep', 0, 0, tiled=True)

time: 787 us -> 636 us (0.81)
  waiting for transfers between devices: 548 us -> 179 us
  Pallas kernels: 125 us -> 406 us
  matrix products: 55.4 us -> 4.24 us
  blocking collectives: 9.49 us -> 0 us
    all_gather x4 -> x0, waiting for transfers between devices: 373 us -> none  [gather_rows(): return lax.all_gather(piece, ('ep', 'dp'), axis=0, tiled=True)]
    pallas_call x0 -> x1, Pallas kernels: none -> 278 us  [attend(): pl.pallas_call(functools.partial(attend_kernel, mesh_n, seq_len), in_spec...]
    dot_general x4 -> x0, matrix products: 50.9 us -> none  [the longest x1 14.5 us: attention_layer(): jnp.einsum('bqhk,bshk->bhqs', query, keys, preferred_element_type=jnp.flo...]
    all_to_all x1 -> x0, blocking collectives: 9.49 us -> none  [local_layer(): lax.all_to_all(slots.T.reshape(n, owned, toks), 'ep', 0, 0, tiled=True)]
    sub x1 -> x0, other arithmetic: 9.13 us -> none  [attention_layer(): jax.nn.softmax(jnp.where(causal, scores, -jnp.inf), axis=-1)]
  transfers between devices with their start and end apart: 7 -> 4, of which waited for: 6 -> 3; matrix products, arithmetic and copies ran while one was open for 8% -> 1% of each run, Pallas kernels for 11% -> 15%
where the time goes in v2:
time: 636 us; the launch traced here: 635 us
  Pallas kernels  406 us (64%)
  waiting for transfers between devices  179 us (28%)
  between operations  13.5 us (2%)
  other arithmetic  11.9 us (2%)
  local copies, waits for them, and re-layouts  11.2 us (2%)
  starting transfers between devices  8.87 us (1%)
    pallas_call x1, Pallas kernels, attend(): pl.pallas_call(functools.partial(attend_kernel, mesh_n, seq_len), in_spec...  278 us
    reduce_scatter x1, waiting for transfers between devices, local_layer(): mixed = lax.psum_scatter(partial, 'ep', scatter_dimension=0, tiled=True)  128 us
    pallas_call x1, Pallas kernels, ffn(): pl.pallas_call(ffn_kernel, grid_spec=pltpu.PrefetchScalarGridSpec(num_sca...  72.5 us
    all_gather x1, waiting for transfers between devices, local_layer(): u_all = lax.all_gather(normed, 'ep', axis=0, tiled=True)  48.1 us
    pallas_call x1, Pallas kernels, combine(): pl.pallas_call(combine_kernel, grid=(n,), in_specs=[table, table, pl.Bloc...  35.8 us
    pallas_call x1, Pallas kernels, dispatch(): pl.pallas_call(dispatch_kernel, grid=(n,), in_specs=[pl.BlockSpec((1, own...  20.3 us
  transfers between devices with their start and end apart: 4, of which 3 were waited for; matrix products, arithmetic and copies ran while one was open for 1% of the time, Pallas kernels for 15%

profile of v2, /device:TPU:81, one launch (start us, length us, event | category | flops | bytes accessed | tf_op | source)
XLA Modules:
  0.0 635.0 jit_solution(8039195321641878900)
XLA Ops:
  6.5 0.0 copy-start
  6.6 0.0 all-gather.2.cloned.1.call-start
  6.6 0.0 copy-start.3
  6.6 0.0 copy-start.4
  6.6 4.1 copy.23
  10.6 0.0 copy-done.3
  10.6 0.0 copy-done.4
  10.6 6.1 copy_bitcast_fusion
  16.8 277.8 %attend.1 = (bf16[384,2048]{1,0:T(8,128)(2,1)}, bf16[8,256,4096]{2,1,0:T(8,128)(2,1)}, bf16[8,256,4096]{2,1,0:T(8,128)(2,1)}, bf16[8,256,4096]{2,1,0:T(8,128)(2,1)}, bf16[8,512,2048]{2,1,0:T(8,128)(2,1)}) custom-call(bf16[384,2048]{1,0:T(8,128)(2,1)} %bitcast.34, bf16[256,4096]{1,0:T(8,128)(2,1)} %bitcast.30, bf16[256,4096]{1,0:T(8,128)(2,1)} %get-tuple-element.10.wk_ref, ...), custom_call_target="tpu_custom_call" | custom-call | flops 25769803776 | bytes 200000000 | tf_op jit(solution)/shard_map/attend/pallas_call | solution.py:206
  294.6 0.0 copy-start.7
  294.6 1.8 fusion.2
  296.4 0.0 copy-start.2
  296.4 3.0 fusion
  299.4 0.1 all-gather.2.cloned.1.call-update
  299.5 0.0 copy-done.7
  299.5 0.1 copy.12
  299.6 2.0 fusion.5
  301.6 0.1 copy.13
  301.8 0.9 fusion.6
  302.7 4.1 all-to-all-start
  306.8 0.0 copy-done
  306.8 0.0 copy-done.2
  306.8 3.3 select_reduce_fusion.1
  310.1 0.1 select_reduce_fusion
  310.2 0.7 fusion.10
  310.9 3.0 all-to-all-done.pos_ref
  313.9 0.0 copy-start.5
  313.9 4.8 all-to-all-start.1
  318.7 0.0 reduce-scatter.2.cloned.1.call-start
  318.7 0.1 reduce_max.19
  318.9 0.6 fusion.12.need_ref
  319.5 48.1 %all-gather.2.cloned.1.call-done.u_ref = bf16[3072,2048]{1,0:T(8,128)(2,1)} async-done(((bf16[384,2048]{1,0:T(8,128)(2,1)}), bf16[3072,2048]{1,0:T(8,128)(2,1)}) %all-gather.2.cloned.1.call-update) | async-done | bytes 12582928 | tf_op jit(solution)/shard_map/all_gather | solution.py:379
  367.5 0.0 copy-done.5
  367.5 20.3 %dispatch.1.rows_ref = bf16[16,3,8,16,2048]{4,3,2,1,0:T(8,128)(2,1)} custom-call(s32[8,16,384]{2,1,0:T(8,128)} %copy-done.5, bf16[3072,2048]{1,0:T(8,128)(2,1)} %all-gather.2.cloned.1.call-done.u_ref), custom_call_target="tpu_custom_call" | custom-call | flops 9663676416 | bytes 40000000 | tf_op jit(solution)/shard_map/dispatch/pallas_call | solution.py:262
  387.8 72.5 %ffn.1.done_ref = bf16[16,3,8,16,2048]{4,3,2,1,0:T(8,128)(2,1)} custom-call(s32[16]{0:T(128)} %fusion.12.need_ref, bf16[16,3,8,16,2048]{4,3,2,1,0:T(8,128)(2,1)} %dispatch.1.rows_ref, bf16[16,2048,768]{2,1,0:T(8,128)(2,1)} %one_ref.1, bf16[16,2048,768]{2,1,0:T(8,128)(2,1)} %three_ref.1, bf16[16,768,2048]{2,1,0:T(8,128)(2,1)} %two_ref.1), custom_call_target="tpu_custom_call" | custom-call | flops 57982058496 | bytes 200000000 | tf_op jit(solution)/shard_map/ffn/pallas_call | solution.py:298
  460.3 0.0 all-to-all-done.1.gate_ref
  460.3 0.0 copy-start.6
  460.3 0.7 copy-done.6
  461.0 35.8 %combine.1 = f32[3072,2048]{1,0:T(8,128)} custom-call(s32[8,16,384]{2,1,0:T(8,128)} %copy-done.5, f32[8,16,384]{2,1,0:T(8,128)} %copy-done.6, bf16[16,3,8,16,2048]{4,3,2,1,0:T(8,128)(2,1)} %ffn.1.done_ref), custom_call_target="tpu_custom_call" | custom-call | flops 28991029248 | bytes 60000000 | tf_op jit(solution)/shard_map/combine/pallas_call | solution.py:346
  496.7 0.1 reduce-scatter.2.cloned.1.call-update
  496.8 0.0 copy-start.1
  496.8 127.8 %reduce-scatter.2.cloned.1.call-done = f32[384,2048]{1,0:T(8,128)} async-done(((f32[3072,2048]{1,0:T(8,128)}), f32[384,2048]{1,0:T(8,128)}) %reduce-scatter.2.cloned.1.call-update) | async-done | bytes 3145744 | tf_op jit(solution)/shard_map/reduce_scatter | solution.py:384
  624.6 3.5 fusion.3
  628.1 0.0 copy-done.1
  (1 shorter events, 0.0 us)
Async XLA Ops:
  6.5 300.3 %copy-start = (f32[2048,128]{1,0:T(8,128)S(1)}, f32[2048,128]{1,0:T(8,128)}, u32[]{:S(2)}) copy-start(f32[2048,128]{1,0:T(8,128)} %param.15) | copy-start | bytes 3145732
  6.6 361.0 %all-gather.2.cloned.1.call-start = ((), (), s32[]{:S(2)}) async-start(), calls=%async_computation.3 | async-start | bytes 14155776 | tf_op jit(solution)/shard_map/all_gather | solution.py:379
  6.6 4.1 copy-start.3
  6.6 4.1 copy-start.4
  294.6 4.9 copy-start.7
  296.4 10.4 %copy-start.2 = (bf16[384,2048]{1,0:T(8,128)(2,1)S(1)}, bf16[384,2048]{1,0:T(8,128)(2,1)}, u32[]{:S(2)}) copy-start(bf16[384,2048]{1,0:T(8,128)(2,1)} %get-tuple-element.6) | copy-start | bytes 4718596
  302.7 11.2 %all-to-all-start = ((s32[8,16,384]{2,1,0:T(8,128)}), s32[8,16,384]{2,1,0:T(8,128)S(1)}, u32[]{:S(2)}, u32[]{:S(2)}) async-start(s32[8,16,384]{2,1,0:T(8,128)} %bitcast.3), calls=%async_computation | async-start | bytes 393216 | tf_op jit(solution)/shard_map/all_to_all | solution.py:373
  313.9 53.6 %copy-start.5 = (s32[8,16,384]{2,1,0:T(8,128)}, s32[8,16,384]{2,1,0:T(8,128)S(1)}, u32[]{:S(2)}) copy-start(s32[8,16,384]{2,1,0:T(8,128)S(1)} %all-to-all-done.pos_ref) | copy-start | bytes 589828
  313.9 146.3 %all-to-all-start.1 = ((f32[8,16,384]{2,1,0:T(8,128)}), f32[8,16,384]{2,1,0:T(8,128)S(1)}, u32[]{:S(2)}, u32[]{:S(2)}) async-start(f32[8,16,384]{2,1,0:T(8,128)} %bitcast.5), calls=%async_computation.1 | async-start | bytes 393216 | tf_op jit(solution)/shard_map/all_to_all | solution.py:380
  318.7 305.9 %reduce-scatter.2.cloned.1.call-start = ((), (), s32[]{:S(2)}) async-start(), calls=%async_computation.4 | async-start | bytes 28311552 | tf_op jit(solution)/shard_map/reduce_scatter | solution.py:384
  460.3 0.7 copy-start.6
  496.8 131.3 %copy-start.1 = (f32[2048,128]{1,0:T(8,128)S(1)}, f32[2048,128]{1,0:T(8,128)}, u32[]{:S(2)}) copy-start(f32[2048,128]{1,0:T(8,128)} %param.15) | copy-start | bytes 3145732
Sparse Core Ops, SparseCore 0:
  299.6 67.9 all-gather.1
  496.9 127.6 reduce-scatter.1

commit v3 on v2

--- a/solution.py
+++ b/solution.py
@@ -18,7 +18,7 @@
 
 
 def attend_kernel(mesh_n, seq_len, x_ref, wq_ref, wk_ref, wv_ref, wo_ref, h_ref, fq_ref, fk_ref, fv_ref, fo_ref,
-                  n_ref, q_ref, k_ref, v_ref, wide_ref, tall_ref, send, recv, load_sem):
+                  n_ref, q_ref, k_ref, v_ref, wide_ref, tall_ref, sum_ref, send, recv, load_sem):
     me = lax.axis_index('ep')
     dp = lax.axis_index('dp')
     core = me % 2
@@ -88,15 +88,21 @@
     def own(m):
         start(m, 0, 2, 1, 3, 9)
 
-    def near(m):
+    def near_first(m):
         arrived(m, 0)
         start(m, 4, 6)
         arrived(m, 2)
         start(m, 5)
+
+    def near_last(m):
         arrived(m, 1)
         start(m, 10)
         arrived(m, 3)
         start(m, 7, 11)
+
+    def near(m):
+        near_first(m)
+        near_last(m)
 
     def far(m):
         arrived(m, 4)
@@ -104,13 +110,13 @@
         arrived(m, 5)
         start(m, 12)
 
-    def zside(m):
-        for slot in (6, 7, 8):
+    def zside(m, slots=(6, 7, 8)):
+        for slot in slots:
             arrived(m, slot)
             start(m, slot + 7)
 
-    def finish(m):
-        for slot in range(9, 16):
+    def finish(m, slots=tuple(range(9, 16))):
+        for slot in slots:
             arrived(m, slot)
 
     def stream(m, buf, width, body):
@@ -170,27 +176,55 @@
     finish(0)
     project(0, q_ref)
     near(2)
+    own(3)
     far(1)
     zside(1)
     finish(1)
-    own(3)
     project(1, k_ref)
     far(2)
     zside(2)
     finish(2)
+    near_first(3)
     project(2, v_ref)
     pairs = q_ref.shape[1] // head_dim // 2
     attention(0, pairs // 2)
-    near(3)
+    near_last(3)
     attention(pairs // 2, pairs)
+    zside(3, (6, 7))
+    finish(3, (9, 10, 11, 13, 14))
+
+    fore, back = ways(3)
+    def twin(source):
+        return source + 1 - 2 * core
+    depth = fo_ref.shape[1]
+    order = (me, sibling, back, fore, twin(back), twin(fore), across, twin(across))
+    def fetch(i):
+        source = wo_ref if i == 0 else fo_ref.at[order[i]]
+        pltpu.make_async_copy(source, tall_ref.at[i % 2], load_sem.at[i % 2]).start()
+    def gather_product(first, last):
+        fetch(first)
+        for i in range(first, last):
+            if i + 1 < last:
+                fetch(i + 1)
+            pltpu.make_async_copy(fo_ref.at[order[i]], tall_ref.at[i % 2], load_sem.at[i % 2]).wait()
+            heads = pl.ds(pl.multiple_of(order[i] * depth, depth), depth)
+            width = min(512, sum_ref.shape[1])
+            def part(c, carry):
+                cols = pl.ds(pl.multiple_of(c * width, width), width)
+                product = jnp.dot(q_ref[:, heads], tall_ref[i % 2, :, cols], preferred_element_type=jnp.float32)
+                if i == 0:
+                    sum_ref[:, cols] = x_ref[:, cols].astype(jnp.float32) + product
+                elif i < mesh_n - 1:
+                    sum_ref[:, cols] += product
+                else:
+                    h_ref[:, cols] = (sum_ref[:, cols] + product).astype(jnp.bfloat16)
+                return carry
+            lax.fori_loop(0, sum_ref.shape[1] // width, part, 0)
+    gather_product(0, mesh_n - 2)
     far(3)
-    zside(3)
-    finish(3)
-
-    def out_body(cols, chunk):
-        mixed = jnp.dot(q_ref[...], chunk, preferred_element_type=jnp.float32)
-        h_ref[:, cols] = (x_ref[:, cols].astype(jnp.float32) + mixed).astype(jnp.bfloat16)
-    stream(3, tall_ref, tall_ref.shape[3], out_body)
+    zside(3, (8,))
+    finish(3, (12, 15))
+    gather_product(mesh_n - 2, mesh_n)
     for m in range(4):
         for slot in range(16):
             outgoing(m, slot).wait_send()
@@ -214,7 +248,8 @@
             pltpu.VMEM((toks, width), bf),
             pltpu.VMEM((toks, width), bf),
             pltpu.VMEM((2, mesh_n, wq.shape[0], min(512, width)), bf),
-            pltpu.VMEM((2, mesh_n, wo.shape[0], min(256, dim)), bf),
+            pltpu.VMEM((2,) + wo.shape, bf),
+            pltpu.VMEM((toks, dim), jnp.float32),
             pltpu.SemaphoreType.DMA((4, 16)),
             pltpu.SemaphoreType.DMA((4, 16)),
             pltpu.SemaphoreType.DMA((2,)),
@@ -242,34 +277,159 @@
     return normed.astype(jnp.bfloat16), grown / jnp.sum(grown, axis=1, keepdims=True)
 
 
-def dispatch_kernel(pos_ref, u_ref, out_ref, hot_ref):
-    owned, toks = pos_ref.shape[1], pos_ref.shape[2]
-    parts = out_ref.shape[1]
+def neighbours(mesh_n):
+    me = lax.axis_index('ep')
+    core = me % 2
+    sibling = me + 1 - 2 * core
+    return me, core, sibling, (me + 2) % mesh_n, (me + mesh_n - 2) % mesh_n, (me + mesh_n // 2) % mesh_n
+
+
+def meet(mesh_n, me):
+    barrier = pltpu.get_barrier_semaphore()
+    for j in range(1, mesh_n):
+        pl.semaphore_signal(barrier, inc=1, device_id={'ep': (me + j) % mesh_n}, device_id_type=MESH)
+    pl.semaphore_wait(barrier, mesh_n - 1)
+
+
+def route_kernel(mesh_n, u_ref, mine_ref, rows_ref, tab_ref, all_ref, hot_ref, stage_ref, send, recv, tab_send, tab_recv, out_sem):
+    me, core, sibling, right, left, across = neighbours(mesh_n)
+    meet(mesh_n, me)
+    toks = u_ref.shape[0]
+    half = toks // 2
+    lows, highs = pl.ds(0, half), pl.ds(half, half)
+
+    def copy(slot, src, dst, peer):
+        return pltpu.make_async_remote_copy(src_ref=src, dst_ref=dst, send_sem=send.at[slot], recv_sem=recv.at[slot],
+                                            device_id={'ep': peer}, device_id_type=MESH)
+
+    def outgoing(slot):
+        if slot < 4:
+            rows = (lows, highs, highs, lows)[slot]
+            return copy(slot, u_ref.at[rows], all_ref.at[me, rows], right if slot < 2 else left)
+        if slot == 4:
+            return copy(slot, all_ref.at[left, lows], all_ref.at[left, lows], right)
+        if slot == 5:
+            return copy(slot, all_ref.at[right, highs], all_ref.at[right, highs], left)
+        if slot == 6:
+            return copy(slot, u_ref, all_ref.at[me], sibling)
+        if slot < 9:
+            source = left if slot == 7 else right
+            return copy(slot, all_ref.at[source], all_ref.at[source], sibling)
+        rows = lows if slot == 9 else highs
+        return copy(slot, all_ref.at[across, rows], all_ref.at[across, rows], sibling)
+
+    def arrived(*slots):
+        for slot in slots:
+            if slot < 4:
+                dst = all_ref.at[left if slot < 2 else right, (lows, highs, highs, lows)[slot]]
+            elif slot < 6:
+                dst = all_ref.at[across, lows if slot == 4 else highs]
+            elif slot == 6:
+                dst = all_ref.at[sibling]
+            elif slot < 9:
+                dst = all_ref.at[(left if slot == 7 else right) + 1 - 2 * core]
+            else:
+                dst = all_ref.at[across + 1 - 2 * core, lows if slot == 9 else highs]
+            copy(slot, dst, dst, sibling).wait_recv()
+
+    def table(j, src, dst, peer):
+        return pltpu.make_async_remote_copy(src_ref=src, dst_ref=dst, send_sem=tab_send.at[j], recv_sem=tab_recv.at[j],
+                                            device_id={'ep': peer}, device_id_type=MESH)
+
+    def table_out(j):
+        peer = (me + j) % mesh_n
+        return table(j, mine_ref.at[peer], tab_ref.at[me], peer)
+
+    for j in range(1, mesh_n):
+        table_out(j).start()
+    for slot in (0, 2, 1, 3, 6):
+        outgoing(slot).start()
+    tab_ref[pl.ds(me, 1)] = mine_ref[pl.ds(me, 1)]
+    for j in range(1, mesh_n):
+        source = (me + mesh_n - j) % mesh_n
+        table(j, tab_ref.at[source], tab_ref.at[source], source).wait_recv()
+
+    owned = tab_ref.shape[1] // 2
+    parts = rows_ref.shape[1]
     cap = parts * SLOT
-    lane = lax.broadcasted_iota(jnp.int32, (cap, toks), 0)
-    for e in range(owned):
-        hot_ref[e * cap:(e + 1) * cap, :] = jnp.where(lane == pos_ref[0, e:e + 1, :], 1.0, 0.0).astype(jnp.bfloat16)
-    width = 512
-    for c in range(u_ref.shape[1] // width):
-        cols = slice(c * width, (c + 1) * width)
-        rows = jnp.dot(hot_ref[...], u_ref[:, cols], preferred_element_type=jnp.float32).astype(jnp.bfloat16)
-        out_ref[:, :, 0, :, cols] = rows.reshape(owned, parts, SLOT, width)
-
-
-def dispatch(pos, u_all, parts):
-    n, owned, toks = pos.shape
-    dim = u_all.shape[1]
+    dim = u_ref.shape[1]
+    width = min(512, dim)
+    lane = lax.broadcasted_iota(jnp.int32, (cap, toks), 0).astype(jnp.float32)
+
+    def flush(k, s):
+        return pltpu.make_async_copy(stage_ref.at[k % 2], rows_ref.at[:, :, s], out_sem.at[k % 2])
+
+    def send_rows(k, s, own=False):
+        pos = tab_ref[pl.ds(s, 1), :owned][0]
+        for e in range(owned):
+            hot_ref[e * cap:(e + 1) * cap, :] = jnp.where(lane == pos[e:e + 1, :], 1.0, 0.0).astype(jnp.bfloat16)
+        if k >= 2:
+            flush(k, s).wait()
+        def part(c, carry):
+            cols = pl.ds(pl.multiple_of(c * width, width), width)
+            block = u_ref[:, cols] if own else all_ref[pl.ds(s, 1), :, cols][0]
+            rows = jnp.dot(hot_ref[...], block, preferred_element_type=jnp.float32).astype(jnp.bfloat16)
+            stage_ref[k % 2, :, :, :, cols] = rows.reshape(owned, parts, SLOT, width)
+            return carry
+        lax.fori_loop(0, dim // width, part, 0)
+        flush(k, s).start()
+
+    send_rows(0, me, True)
+    arrived(6)
+    send_rows(1, sibling)
+    arrived(0)
+    outgoing(4).start()
+    arrived(2)
+    outgoing(5).start()
+    arrived(1)
+    outgoing(7).start()
+    arrived(3)
+    outgoing(8).start()
+    send_rows(2, left)
+    send_rows(3, right)
+    arrived(7)
+    send_rows(4, left + 1 - 2 * core)
+    arrived(8)
+    send_rows(5, right + 1 - 2 * core)
+    arrived(4)
+    outgoing(9).start()
+    arrived(5)
+    outgoing(10).start()
+    send_rows(6, across)
+    arrived(9, 10)
+    send_rows(7, across + 1 - 2 * core)
+    flush(6, me).wait()
+    flush(7, me).wait()
+    for j in range(1, mesh_n):
+        table_out(j).wait_send()
+    for slot in range(11):
+        outgoing(slot).wait_send()
+
+
+def route(mesh_n, u, table, parts):
+    toks, dim = u.shape
+    owned = table.shape[1] // 2
+    bf = jnp.bfloat16
+    vmem = pl.BlockSpec(memory_space=pltpu.VMEM)
     return pl.pallas_call(
-        dispatch_kernel,
-        grid=(n,),
-        in_specs=[pl.BlockSpec((1, owned, toks), lambda s: (s, 0, 0)), pl.BlockSpec((toks, dim), lambda s: (s, 0))],
-        out_specs=pl.BlockSpec((owned, parts, 1, SLOT, dim), lambda s: (0, 0, s, 0, 0)),
-        out_shape=jax.ShapeDtypeStruct((owned, parts, n, SLOT, dim), jnp.bfloat16),
-        scratch_shapes=[pltpu.VMEM((owned * parts * SLOT, toks), jnp.bfloat16)],
-        compiler_params=pltpu.CompilerParams(vmem_limit_bytes=60 * 2 ** 20),
-        cost_estimate=pl.CostEstimate(flops=2 * n * owned * parts * SLOT * toks * dim, bytes_accessed=40_000_000, transcendentals=0),
-        name="dispatch",
-    )(pos, u_all)
+        functools.partial(route_kernel, mesh_n),
+        in_specs=[vmem, vmem],
+        out_specs=[pl.BlockSpec(memory_space=pltpu.HBM), vmem],
+        out_shape=[jax.ShapeDtypeStruct((owned, parts, mesh_n, SLOT, dim), bf), jax.ShapeDtypeStruct(table.shape, jnp.float32)],
+        scratch_shapes=[
+            pltpu.VMEM((mesh_n, toks, dim), bf),
+            pltpu.VMEM((owned * parts * SLOT, toks), bf),
+            pltpu.VMEM((2, owned, parts, SLOT, dim), bf),
+            pltpu.SemaphoreType.DMA((11,)),
+            pltpu.SemaphoreType.DMA((11,)),
+            pltpu.SemaphoreType.DMA((mesh_n,)),
+            pltpu.SemaphoreType.DMA((mesh_n,)),
+            pltpu.SemaphoreType.DMA((2,)),
+        ],
+        compiler_params=pltpu.CompilerParams(collective_id=1, has_side_effects=True, vmem_limit_bytes=56 * 2 ** 20),
+        cost_estimate=pl.CostEstimate(flops=2 * mesh_n * owned * parts * SLOT * toks * dim, bytes_accessed=40_000_000, transcendentals=0),
+        name='route',
+    )(u, table)
 
 
 def ffn_kernel(need_ref, rows_ref, one_ref, three_ref, two_ref, out_ref):
@@ -315,45 +475,124 @@
     )(need, rows, w_one, w_three, w_two)
 
 
-def combine_kernel(pos_ref, gate_ref, done_ref, out_ref, big_ref, mid_ref, low_ref):
-    owned, toks = pos_ref.shape[1], pos_ref.shape[2]
+def settle_kernel(mesh_n, tab_ref, h_ref, done_ref, y_ref, big_ref, mid_ref, low_ref, load_ref, pass_ref, twin_ref, sum_ref, far_ref, near_ref,
+                  load_sem, twin_send, twin_recv, send, recv):
+    me, core, sibling, right, left, across = neighbours(mesh_n)
+    meet(mesh_n, me)
+    toks, dim = h_ref.shape
+    half = toks // 2
+    lows, highs = slice(0, half), slice(half, toks)
+    owned = tab_ref.shape[1] // 2
     parts = done_ref.shape[1]
     cap = parts * SLOT
-    lane = lax.broadcasted_iota(jnp.int32, (cap, toks), 0)
-    gate = gate_ref[0]
-    big = gate.astype(jnp.bfloat16).astype(jnp.float32)
-    mid = (gate - big).astype(jnp.bfloat16).astype(jnp.float32)
-    low = (gate - big) - mid
-    for e in range(owned):
-        here = lane == pos_ref[0, e:e + 1, :]
-        rows = slice(e * cap, (e + 1) * cap)
-        for ref, part in ((big_ref, big), (mid_ref, mid), (low_ref, low)):
-            ref[rows, :] = jnp.where(here, part[e:e + 1, :], 0.0).astype(jnp.bfloat16)
-    width = 512
+    width = min(512, dim)
+    lane = lax.broadcasted_iota(jnp.int32, (cap, toks), 0).astype(jnp.float32)
     over = (((0,), (0,)), ((), ()))
-    for c in range(out_ref.shape[1] // width):
-        cols = slice(c * width, (c + 1) * width)
-        done = done_ref[:, :, 0, :, cols].reshape(owned * cap, width)
-        total = lax.dot_general(low_ref[...], done, over, preferred_element_type=jnp.float32)
-        total += lax.dot_general(mid_ref[...], done, over, preferred_element_type=jnp.float32)
-        out_ref[:, cols] = total + lax.dot_general(big_ref[...], done, over, preferred_element_type=jnp.float32)
-
-
-def combine(pos, gates, done):
-    n, owned, toks = pos.shape
-    parts, dim = done.shape[1], done.shape[4]
-    table = pl.BlockSpec((1, owned, toks), lambda s: (s, 0, 0))
+    chips = (across, right, left, me)
+    jobs = [dest for chip in chips for dest in (chip + 1 - 2 * core, chip)]
+
+    def fetch(k):
+        return pltpu.make_async_copy(done_ref.at[:, :, jobs[k]], load_ref.at[k % 2], load_sem.at[k % 2])
+
+    def partial(k, out, index):
+        tab = tab_ref[pl.ds(jobs[k], 1)][0]
+        pos, gate = tab[:owned], tab[owned:]
+        big = gate.astype(jnp.bfloat16).astype(jnp.float32)
+        mid = (gate - big).astype(jnp.bfloat16).astype(jnp.float32)
+        low = (gate - big) - mid
+        for e in range(owned):
+            here = lane == pos[e:e + 1, :]
+            for ref, piece in ((big_ref, big), (mid_ref, mid), (low_ref, low)):
+                ref[e * cap:(e + 1) * cap, :] = jnp.where(here, piece[e:e + 1, :], 0.0).astype(jnp.bfloat16)
+        fetch(k).wait()
+        if k + 1 < len(jobs):
+            fetch(k + 1).start()
+        def part(c, carry):
+            cols = pl.ds(pl.multiple_of(c * width, width), width)
+            block = load_ref[k % 2, :, :, :, cols].reshape(owned * cap, width)
+            total = lax.dot_general(low_ref[...], block, over, preferred_element_type=jnp.float32)
+            total += lax.dot_general(mid_ref[...], block, over, preferred_element_type=jnp.float32)
+            out[index, :, cols] = total + lax.dot_general(big_ref[...], block, over, preferred_element_type=jnp.float32)
+            return carry
+        lax.fori_loop(0, dim // width, part, 0)
+
+    def twin(i):
+        return pltpu.make_async_remote_copy(src_ref=pass_ref.at[i % 2], dst_ref=twin_ref.at[i], send_sem=twin_send.at[i],
+                                            recv_sem=twin_recv.at[i], device_id={'ep': sibling}, device_id_type=MESH)
+
+    def hop(slot):
+        if slot < 2:
+            src, dst = sum_ref.at[0, (lows, highs)[slot]], far_ref.at[slot]
+        else:
+            rows = (lows, highs)[slot % 2]
+            src, dst = sum_ref.at[slot // 2, rows], near_ref.at[slot // 2 - 1, rows]
+        return pltpu.make_async_remote_copy(src_ref=src, dst_ref=dst, send_sem=send.at[slot], recv_sem=recv.at[slot],
+                                            device_id={'ep': (right, left, right, right, left, left)[slot]}, device_id_type=MESH)
+
+    fetch(0).start()
+    for i in range(4):
+        if i >= 2:
+            twin(i - 2).wait_send()
+        partial(2 * i, pass_ref, i % 2)
+        twin(i).start()
+        partial(2 * i + 1, sum_ref, i)
+        twin(i).wait_recv()
+        sum_ref[i] += twin_ref[i]
+        if i == 0:
+            hop(0).start()
+            hop(1).start()
+        if i == 1:
+            hop(3).start()
+        if i == 2:
+            hop(4).start()
+    hop(0).wait_recv()
+    sum_ref[1, lows] += far_ref[0]
+    hop(2).start()
+    hop(1).wait_recv()
+    sum_ref[2, highs] += far_ref[1]
+    hop(5).start()
+    sum_ref[3] += h_ref[...].astype(jnp.float32)
+    hop(3).wait_recv()
+    sum_ref[3, highs] += near_ref[0, highs]
+    hop(4).wait_recv()
+    sum_ref[3, lows] += near_ref[1, lows]
+    hop(2).wait_recv()
+    y_ref[lows] = (sum_ref[3, lows] + near_ref[0, lows]).astype(jnp.bfloat16)
+    hop(5).wait_recv()
+    y_ref[highs] = (sum_ref[3, highs] + near_ref[1, highs]).astype(jnp.bfloat16)
+    for i in (2, 3):
+        twin(i).wait_send()
+    for slot in range(6):
+        hop(slot).wait_send()
+
+
+def settle(mesh_n, table, h, done):
+    toks, dim = h.shape
+    owned, parts = done.shape[:2]
+    bf, f32 = jnp.bfloat16, jnp.float32
+    vmem = pl.BlockSpec(memory_space=pltpu.VMEM)
     return pl.pallas_call(
-        combine_kernel,
-        grid=(n,),
-        in_specs=[table, table, pl.BlockSpec((owned, parts, 1, SLOT, dim), lambda s: (0, 0, s, 0, 0))],
-        out_specs=pl.BlockSpec((toks, dim), lambda s: (s, 0)),
-        out_shape=jax.ShapeDtypeStruct((n * toks, dim), jnp.float32),
-        scratch_shapes=[pltpu.VMEM((owned * parts * SLOT, toks), jnp.bfloat16)] * 3,
-        compiler_params=pltpu.CompilerParams(vmem_limit_bytes=60 * 2 ** 20),
-        cost_estimate=pl.CostEstimate(flops=6 * n * owned * parts * SLOT * toks * dim, bytes_accessed=60_000_000, transcendentals=0),
-        name="combine",
-    )(pos, gates, done)
+        functools.partial(settle_kernel, mesh_n),
+        in_specs=[vmem, vmem, pl.BlockSpec(memory_space=pltpu.HBM)],
+        out_specs=vmem,
+        out_shape=jax.ShapeDtypeStruct((toks, dim), bf),
+        scratch_shapes=[pltpu.VMEM((owned * parts * SLOT, toks), bf)] * 3 + [
+            pltpu.VMEM((2, owned, parts, SLOT, dim), bf),
+            pltpu.VMEM((2, toks, dim), f32),
+            pltpu.VMEM((4, toks, dim), f32),
+            pltpu.VMEM((4, toks, dim), f32),
+            pltpu.VMEM((2, toks // 2, dim), f32),
+            pltpu.VMEM((2, toks, dim), f32),
+            pltpu.SemaphoreType.DMA((2,)),
+            pltpu.SemaphoreType.DMA((4,)),
+            pltpu.SemaphoreType.DMA((4,)),
+            pltpu.SemaphoreType.DMA((6,)),
+            pltpu.SemaphoreType.DMA((6,)),
+        ],
+        compiler_params=pltpu.CompilerParams(collective_id=2, has_side_effects=True, vmem_limit_bytes=60 * 2 ** 20),
+        cost_estimate=pl.CostEstimate(flops=6 * mesh_n * owned * parts * SLOT * toks * dim, bytes_accessed=60_000_000, transcendentals=0),
+        name='settle',
+    )(table, h, done)
 
 
 def solution(mesh):
@@ -370,19 +609,14 @@
         parts = 2 * toks * choices // experts // SLOT
 
         member, slots = slot_table(expert_ids.reshape(toks, choices), experts)
-        pos = lax.all_to_all(slots.T.reshape(n, owned, toks), 'ep', 0, 0, tiled=True)
-        need = jnp.max(pos, axis=(0, 2)) // SLOT + 1
-
         flat = [w.reshape(w.shape[0], -1) for w in (w_query, w_key, w_value, w_out)]
         hidden = attend(n, seq_len, tokens.reshape(toks, model_dim), *flat)
         normed, gates_local = dense_gates(hidden, w_router, member)
-        u_all = lax.all_gather(normed, 'ep', axis=0, tiled=True)
-        gates = lax.all_to_all(gates_local.T.reshape(n, owned, toks), 'ep', 0, 0, tiled=True)
-        rows = dispatch(pos, u_all, parts)
+        mine = jnp.concatenate([slots.astype(jnp.float32).T.reshape(n, owned, toks), gates_local.T.reshape(n, owned, toks)], axis=1)
+        rows, table = route(n, normed, mine, parts)
+        need = jnp.max(table[:, :owned], axis=(0, 2)).astype(jnp.int32) // SLOT + 1
         done = ffn(need, rows, w_one, w_three, w_two)
-        partial = combine(pos, gates, done)
-        mixed = lax.psum_scatter(partial, 'ep', scatter_dimension=0, tiled=True)
-        layer_out = (hidden.astype(jnp.float32) + mixed).astype(jnp.bfloat16)
+        layer_out = settle(n, table, hidden, done)
         return layer_out.reshape(seq_count, seq_len, model_dim)
 
     return jax.shard_map(local_layer, mesh=mesh, in_specs=(tok_spec, row_spec, row_spec, row_spec, row_spec, P(), row_spec, row_spec, row_spec, tok_spec), out_specs=tok_spec, check_vma=False)

time: 636 us -> 571 us (0.90)
  waiting for transfers between devices: 179 us -> 0 us
  Pallas kernels: 406 us -> 539 us
  between operations: 13.5 us -> 0.54 us
  starting transfers between devices: 8.87 us -> 0 us
    pallas_call x2, Pallas kernels: 56 us -> 193 us  [the longest x1 125 us: settle(): pl.pallas_call(functools.partial(settle_kernel, mesh_n), in_specs=[vmem,...]
    reduce_scatter x1 -> x0, waiting for transfers between devices: 128 us -> none  [local_layer(): mixed = lax.psum_scatter(partial, 'ep', scatter_dimension=0, tiled=True)]
    all_gather x1 -> x0, waiting for transfers between devices: 48.1 us -> none  [local_layer(): u_all = lax.all_gather(normed, 'ep', axis=0, tiled=True)]
    all_to_all x2 -> x0, starting transfers between devices: 8.86 us -> none  [the longest x1 4.79 us: local_layer(): lax.all_to_all(gates_local.T.reshape(n, owned, toks), 'ep', 0, 0, tiled=T...]
  transfers between devices with their start and end apart: 4 -> 0, of which waited for: 3 -> 0; matrix products, arithmetic and copies ran while one was open for 1% -> 0% of each run, Pallas kernels for 15% -> 0%
where the time goes in v3:
time: 571 us; the launch traced here: 564 us
  Pallas kernels  539 us (94%)
  local copies, waits for them, and re-layouts  13.9 us (2%)
  other arithmetic  7.94 us (1%)
    pallas_call x1, Pallas kernels, attend(): pl.pallas_call(functools.partial(attend_kernel, mesh_n, seq_len), in_spec...  277 us
    pallas_call x1, Pallas kernels, settle(): pl.pallas_call(functools.partial(settle_kernel, mesh_n), in_specs=[vmem,...  125 us
    pallas_call x1, Pallas kernels, ffn(): pl.pallas_call(ffn_kernel, grid_spec=pltpu.PrefetchScalarGridSpec(num_sca...  68.7 us
    pallas_call x1, Pallas kernels, route(): pl.pallas_call(functools.partial(route_kernel, mesh_n), in_specs=[vmem, v...  68.6 us

profile of v3, /device:TPU:81, one launch (start us, length us, event | category | flops | bytes accessed | tf_op | source)
XLA Modules:
  0.0 564.5 jit_solution(6327542830182521423)
XLA Ops:
  0.0 0.0 copy-start
  0.0 0.0 copy-start.3
  0.0 8.6 %copy_bitcast_fusion = (bf16[256,4096]{1,0:T(8,128)(2,1)}, bf16[256,4096]{1,0:T(8,128)(2,1)}) fusion(bf16[32,8,32,128]{3,2,1,0:T(8,128)(2,1)} %bitcast.31, bf16[32,8,32,128]{3,2,1,0:T(8,128)(2,1)} %bitcast.32), kind=kLoop, calls=%fused_computation.5 | loop fusion | bytes 8388608 | tf_op jit(solution)/shard_map/reshape | solution.py:612
  8.6 0.0 copy-done.3
  8.6 2.3 copy.23
  10.9 0.0 copy-start.4
  10.9 276.7 %attend.1 = (bf16[384,2048]{1,0:T(8,128)(2,1)}, bf16[8,256,4096]{2,1,0:T(8,128)(2,1)}, bf16[8,256,4096]{2,1,0:T(8,128)(2,1)}, bf16[8,256,4096]{2,1,0:T(8,128)(2,1)}, bf16[8,512,2048]{2,1,0:T(8,128)(2,1)}) custom-call(bf16[384,2048]{1,0:T(8,128)(2,1)} %bitcast.37, bf16[256,4096]{1,0:T(8,128)(2,1)} %bitcast.30, bf16[256,4096]{1,0:T(8,128)(2,1)} %get-tuple-element.14.wk_ref, ...), custom_call_target="tpu_custom_call" | custom-call | flops 25769803776 | bytes 200000000 | tf_op jit(solution)/shard_map/attend/pallas_call | solution.py:240
  287.6 0.0 copy-start.2
  287.6 1.9 fusion.2
  289.5 0.0 copy-done.4
  289.5 0.1 copy.12
  289.6 2.0 fusion.4
  291.7 0.1 copy.13
  291.8 0.0 copy-done
  291.9 0.0 copy-done.2
  291.9 3.3 select_reduce_fusion.1
  295.2 0.1 select_reduce_fusion
  295.2 0.1 fusion.10
  295.3 0.3 fusion.6
  295.6 0.8 pad_maximum_fusion.mine_ref
  296.4 1.5 fusion.1.u_ref
  297.8 68.6 %route.1 = (bf16[16,3,8,16,2048]{4,3,2,1,0:T(8,128)(2,1)}, f32[8,32,384]{2,1,0:T(8,128)}) custom-call(bf16[384,2048]{1,0:T(8,128)(2,1)} %fusion.1.u_ref, f32[8,32,384]{2,1,0:T(8,128)} %pad_maximum_fusion.mine_ref), custom_call_target="tpu_custom_call" | custom-call | flops 9663676416 | bytes 40000000 | tf_op jit(solution)/shard_map/route/pallas_call | solution.py:414
  366.4 1.1 slice_reduce_fusion
  367.5 0.5 fusion.12.need_ref
  368.0 68.7 %ffn.1.done_ref = bf16[16,3,8,16,2048]{4,3,2,1,0:T(8,128)(2,1)} custom-call(s32[16]{0:T(128)} %fusion.12.need_ref, bf16[16,3,8,16,2048]{4,3,2,1,0:T(8,128)(2,1)} %get-tuple-element.10.rows_ref, bf16[16,2048,768]{2,1,0:T(8,128)(2,1)} %one_ref.1, bf16[16,2048,768]{2,1,0:T(8,128)(2,1)} %three_ref.1, bf16[16,768,2048]{2,1,0:T(8,128)(2,1)} %two_ref.1), custom_call_target="tpu_custom_call" | custom-call | flops 57982058496 | bytes 200000000 | tf_op jit(solution)/shard_map/ffn/pallas_call | solution.py:458
  436.7 0.0 copy-start.1
  436.7 124.6 %settle.1 = bf16[384,2048]{1,0:T(8,128)(2,1)} custom-call(f32[8,32,384]{2,1,0:T(8,128)} %get-tuple-element.9.tab_ref, bf16[384,2048]{1,0:T(8,128)(2,1)} %get-tuple-element.8.h_ref, bf16[16,3,8,16,2048]{4,3,2,1,0:T(8,128)(2,1)} %ffn.1.done_ref), custom_call_target="tpu_custom_call" | custom-call | flops 28991029248 | bytes 60000000 | tf_op jit(solution)/shard_map/settle/pallas_call | solution.py:574
  561.3 2.7 copy.29
  564.0 0.0 copy-done.1
  (1 shorter events, 0.0 us)
Async XLA Ops:
  0.0 291.8 %copy-start = (f32[2048,128]{1,0:T(8,128)S(1)}, f32[2048,128]{1,0:T(8,128)}, u32[]{:S(2)}) copy-start(f32[2048,128]{1,0:T(8,128)} %param.15) | copy-start | bytes 3145732
  0.0 8.6 %copy-start.3 = (bf16[256,32,128]{2,1,0:T(8,128)(2,1)S(1)}, bf16[256,32,128]{2,1,0:T(8,128)(2,1)}, u32[]{:S(2)}) copy-start(bf16[256,32,128]{2,1,0:T(8,128)(2,1)} %param.11) | copy-start | bytes 6291460
  10.9 278.6 %copy-start.4 = (s32[3,128,8]{1,2,0:T(8,128)S(1)}, s32[3,128,8]{1,2,0:T(8,128)}, u32[]{:S(2)}) copy-start(s32[3,128,8]{1,2,0:T(8,128)} %param.19) | copy-start | bytes 36868
  287.6 4.3 copy-start.2
  436.7 127.3 %copy-start.1 = (f32[2048,128]{1,0:T(8,128)S(1)}, f32[2048,128]{1,0:T(8,128)}, u32[]{:S(2)}) copy-start(f32[2048,128]{1,0:T(8,128)} %param.15) | copy-start | bytes 3145732

commit v4 on v3

--- a/solution.py
+++ b/solution.py
@@ -9,76 +9,90 @@
 
 EPS = 1e-6
 SLOT = 16
+VMEM_BYTES = 60 * 2 ** 20
+ROWS_BY_ROWS = (((1,), (1,)), ((), ()))
+TALL_BY_TALL = (((0,), (0,)), ((), ()))
 MESH = pl.DeviceIdType.MESH
 
 
-def rms_norm(vals):
-    wide = vals.astype(jnp.float32)
-    return wide * lax.rsqrt(jnp.mean(wide * wide, axis=-1, keepdims=True) + EPS)
-
-
-def attend_kernel(mesh_n, seq_len, x_ref, wq_ref, wk_ref, wv_ref, wo_ref, h_ref, fq_ref, fk_ref, fv_ref, fo_ref,
-                  n_ref, q_ref, k_ref, v_ref, wide_ref, tall_ref, sum_ref, send, recv, load_sem):
+def neighbours(mesh_n):
     me = lax.axis_index('ep')
+    core = me % 2
+    sibling = me + 1 - 2 * core
+    return me, core, sibling, (me + 2) % mesh_n, (me + mesh_n - 2) % mesh_n, (me + mesh_n // 2) % mesh_n
+
+
+def meet(mesh_n, me):
+    barrier = pltpu.get_barrier_semaphore()
+    for j in range(1, mesh_n):
+        pl.semaphore_signal(barrier, inc=1, device_id={'ep': (me + j) % mesh_n}, device_id_type=MESH)
+    pl.semaphore_wait(barrier, mesh_n - 1)
+
+
+def attend_kernel(mesh_n, stride, seq_len, x_ref, wq_ref, wk_ref, wv_ref, wo_ref, h_ref, fq_ref, fk_ref, fv_ref, fo_ref,
+                  n_ref, q_ref, k_ref, wide_ref, tall_ref, sum_ref, send, recv, load_sem):
+    me, core, sibling, right, left, across = neighbours(mesh_n)
     dp = lax.axis_index('dp')
-    core = me % 2
-    odd = dp % 2
-    right = (me + 2) % mesh_n
-    left = (me + mesh_n - 2) % mesh_n
-    across = (me + mesh_n // 2) % mesh_n
-    sibling = me + 1 - 2 * core
-    partner = dp + 1 - 2 * odd
+    zbit, ybit = dp % 2, (dp // stride) % 2
+    zflip, yflip = dp + 1 - 2 * zbit, dp + stride * (1 - 2 * ybit)
+    place = zbit + ybit * (3 - 2 * zbit)
+    after = zflip + (place % 2) * (yflip - zflip)
+    before = yflip + (place % 2) * (zflip - yflip)
     own_refs = (wq_ref, wk_ref, wv_ref, wo_ref)
     full_refs = (fq_ref, fk_ref, fv_ref, fo_ref)
 
     barrier = pltpu.get_barrier_semaphore()
     for peer in (right, left, sibling):
         pl.semaphore_signal(barrier, inc=1, device_id={'ep': peer}, device_id_type=MESH)
-    pl.semaphore_signal(barrier, inc=1, device_id={'dp': partner}, device_id_type=MESH)
-    pl.semaphore_wait(barrier, 4)
-
-    def spans(m):
-        unit = own_refs[m].shape[0] // 16
-        def at(even_off, odd_off, size):
-            return pl.ds(pl.multiple_of((even_off + odd * (odd_off - even_off)) * unit, unit), size * unit)
-        return {'F': at(0, 10, 6), 'S': at(6, 5, 5), 'X': at(0, 5, 11), 'ZS': at(0, 11, 5), 'ZR': at(11, 0, 5)}
+    for peer in (after, before):
+        pl.semaphore_signal(barrier, inc=1, device_id={'dp': peer}, device_id_type=MESH)
+    pl.semaphore_wait(barrier, 5)
+
+    def quarter(m, j):
+        size = own_refs[m].shape[0] // 4
+        return pl.ds(pl.multiple_of((place + j) % 4 * size, size), size)
 
     def ways(m):
         return (right, left) if m % 2 == 0 else (left, right)
+
+    def sources(m):
+        fore, back = ways(m)
+        return back, fore, across
+
+    def twin(source):
+        return source + 1 - 2 * core
 
     def copy(m, slot, src, dst, peer):
         return pltpu.make_async_remote_copy(src_ref=src, dst_ref=dst, send_sem=send.at[m, slot], recv_sem=recv.at[m, slot],
                                             device_id=peer, device_id_type=MESH)
 
     def outgoing(m, slot):
-        full, own, span, (fore, back) = full_refs[m], own_refs[m], spans(m), ways(m)
+        full, own, (fore, back) = full_refs[m], own_refs[m], ways(m)
         if slot < 4:
-            rows = span['FSSF'[slot]]
+            rows = quarter(m, (0, 1, 1, 0)[slot])
             return copy(m, slot, own.at[rows], full.at[me, rows], {'ep': fore if slot < 2 else back})
+        if slot == 12:
+            return copy(m, slot, own, full.at[me], {'ep': sibling})
         if slot < 6:
-            rows, source = (span['F'], back) if slot == 4 else (span['S'], fore)
-            return copy(m, slot, full.at[source, rows], full.at[source, rows], {'ep': fore if slot == 4 else back})
-        if slot < 9:
-            source, rows = (back, fore, across)[slot - 6], span['ZS']
-            return copy(m, slot, full.at[source, rows], full.at[source, rows], {'dp': partner})
-        if slot == 9:
-            return copy(m, slot, own, full.at[me], {'ep': sibling})
-        source, rows = (back, fore, across)[(slot - 10) % 3], span['X' if slot < 13 else 'ZR']
-        return copy(m, slot, full.at[source, rows], full.at[source, rows], {'ep': sibling})
+            source, rows, peer = (back, fore)[slot - 4], quarter(m, slot - 4), {'ep': (fore, back)[slot - 4]}
+        elif slot < 12:
+            source, rows, peer = sources(m)[slot % 3], quarter(m, slot // 9), {'dp': after if slot < 9 else before}
+        else:
+            source, rows, peer = sources(m)[(slot - 13) % 3], quarter(m, (0, 1, 3, 2)[(slot - 13) // 3]), {'ep': sibling}
+        return copy(m, slot, full.at[source, rows], full.at[source, rows], peer)
 
     def arrived(m, slot):
-        full, span, (fore, back) = full_refs[m], spans(m), ways(m)
+        full, (fore, back) = full_refs[m], ways(m)
         if slot < 4:
-            dst = full.at[back if slot < 2 else fore, span['FSSF'[slot]]]
+            dst = full.at[back if slot < 2 else fore, quarter(m, (0, 1, 1, 0)[slot])]
         elif slot < 6:
-            dst = full.at[across, span['F' if slot == 4 else 'S']]
-        elif slot < 9:
-            dst = full.at[(back, fore, across)[slot - 6], span['ZR']]
-        elif slot == 9:
+            dst = full.at[across, quarter(m, slot - 4)]
+        elif slot < 12:
+            dst = full.at[sources(m)[slot % 3], quarter(m, 3 if slot < 9 else 2)]
+        elif slot == 12:
             dst = full.at[sibling]
         else:
-            source = (back, fore, across)[(slot - 10) % 3]
-            dst = full.at[source + 1 - 2 * core, span['X' if slot < 13 else 'ZR']]
+            dst = full.at[twin(sources(m)[(slot - 13) % 3]), quarter(m, (0, 1, 3, 2)[(slot - 13) // 3])]
         copy(m, slot, dst, dst, {'ep': sibling}).wait_recv()
 
     def start(m, *slots):
@@ -86,19 +100,19 @@
             outgoing(m, slot).start()
 
     def own(m):
-        start(m, 0, 2, 1, 3, 9)
+        start(m, 0, 2, 1, 3, 12)
 
     def near_first(m):
         arrived(m, 0)
-        start(m, 4, 6)
+        start(m, 4, 6, 13)
         arrived(m, 2)
-        start(m, 5)
+        start(m, 5, 10, 17)
 
     def near_last(m):
         arrived(m, 1)
-        start(m, 10)
+        start(m, 9, 16)
         arrived(m, 3)
-        start(m, 7, 11)
+        start(m, 7, 14)
 
     def near(m):
         near_first(m)
@@ -106,16 +120,16 @@
 
     def far(m):
         arrived(m, 4)
-        start(m, 8)
+        start(m, 8, 15)
         arrived(m, 5)
-        start(m, 12)
-
-    def zside(m, slots=(6, 7, 8)):
+        start(m, 11, 18)
+
+    def beside(m, slots=(6, 10, 9, 7, 8, 11)):
         for slot in slots:
             arrived(m, slot)
-            start(m, slot + 7)
-
-    def finish(m, slots=tuple(range(9, 16))):
+            start(m, slot + 13)
+
+    def finish(m, slots=tuple(range(12, 25))):
         for slot in slots:
             arrived(m, slot)
 
@@ -149,53 +163,63 @@
     seqs = x_ref.shape[0] // seq_len
     causal = lax.broadcasted_iota(jnp.int32, (seq_len, seq_len), 0) >= lax.broadcasted_iota(jnp.int32, (seq_len, seq_len), 1)
 
-    def attention(first, last):
+    pairs = q_ref.shape[1] // head_dim // 2
+
+    def weigh(first, last):
         def step(i, carry):
             for b in range(seqs):
                 rows = slice(b * seq_len, (b + 1) * seq_len)
                 for j in range(2):
                     cols = pl.ds(pl.multiple_of((2 * i + j) * head_dim, head_dim), head_dim)
-                    scores = lax.dot_general(q_ref[rows, cols], k_ref[rows, cols], (((1,), (1,)), ((), ())),
+                    scores = lax.dot_general(q_ref[rows, cols], k_ref[rows, cols], ROWS_BY_ROWS,
                                              preferred_element_type=jnp.float32) * head_dim ** -0.5
                     scores = jnp.where(causal, scores, -jnp.inf)
                     grown = jnp.exp(scores - jnp.max(scores, axis=1, keepdims=True))
-                    weights = (grown * (1.0 / jnp.sum(grown, axis=1, keepdims=True))).astype(jnp.bfloat16)
-                    q_ref[rows, cols] = jnp.dot(weights, v_ref[rows, cols], preferred_element_type=jnp.float32).astype(jnp.bfloat16)
+                    q_ref[rows, cols] = (grown * (1.0 / jnp.sum(grown, axis=1, keepdims=True))).astype(jnp.bfloat16)
             return carry
         lax.fori_loop(first, last, step, 0)
+
+    def mix(cols, chunk):
+        values = jnp.dot(n_ref[...], chunk, preferred_element_type=jnp.float32).astype(jnp.bfloat16)
+        for j in range(values.shape[1] // head_dim):
+            lanes = slice(j * head_dim, (j + 1) * head_dim)
+            here = pl.ds(pl.multiple_of(cols.start + j * head_dim, head_dim), head_dim)
+            for b in range(seqs):
+                rows = slice(b * seq_len, (b + 1) * seq_len)
+                q_ref[rows, here] = jnp.dot(q_ref[rows, here], values[rows, lanes], preferred_element_type=jnp.float32).astype(jnp.bfloat16)
 
     own(0)
     own(1)
     wide = x_ref[...].astype(jnp.float32)
     n_ref[...] = (wide * lax.rsqrt(jnp.mean(wide * wide, axis=-1, keepdims=True) + EPS)).astype(jnp.bfloat16)
     near(0)
+    near(1)
     own(2)
-    near(1)
     far(0)
-    zside(0)
+    far(1)
+    beside(0)
     finish(0)
     project(0, q_ref)
-    near(2)
+    beside(1)
+    finish(1)
+    near_first(2)
     own(3)
-    far(1)
-    zside(1)
-    finish(1)
     project(1, k_ref)
+    near_last(2)
+    weigh(0, pairs // 2)
     far(2)
-    zside(2)
+    near_first(3)
+    weigh(pairs // 2, pairs)
+    beside(2)
     finish(2)
-    near_first(3)
-    project(2, v_ref)
-    pairs = q_ref.shape[1] // head_dim // 2
-    attention(0, pairs // 2)
+    stream(2, wide_ref, wide_ref.shape[3], mix)
     near_last(3)
-    attention(pairs // 2, pairs)
-    zside(3, (6, 7))
-    finish(3, (9, 10, 11, 13, 14))
+    far(3)
+    late = [slot for slot in range(13, 25) if (slot - 13) % 3 == 2]
+    beside(3, (6, 10, 9, 7))
+    finish(3, [slot for slot in range(12, 25) if slot not in late])
 
     fore, back = ways(3)
-    def twin(source):
-        return source + 1 - 2 * core
     depth = fo_ref.shape[1]
     order = (me, sibling, back, fore, twin(back), twin(fore), across, twin(across))
     def fetch(i):
@@ -221,16 +245,15 @@
                 return carry
             lax.fori_loop(0, sum_ref.shape[1] // width, part, 0)
     gather_product(0, mesh_n - 2)
-    far(3)
-    zside(3, (8,))
-    finish(3, (12, 15))
+    beside(3, (8, 11))
+    finish(3, late)
     gather_product(mesh_n - 2, mesh_n)
     for m in range(4):
-        for slot in range(16):
+        for slot in range(25):
             outgoing(m, slot).wait_send()
 
 
-def attend(mesh_n, seq_len, x, wq, wk, wv, wo):
+def attend(mesh_n, stride, seq_len, x, wq, wk, wv, wo):
     toks, dim = x.shape
     width = wq.shape[1]
     bf = jnp.bfloat16
@@ -238,7 +261,7 @@
     hbm = pl.BlockSpec(memory_space=pltpu.HBM)
     fulls = [jax.ShapeDtypeStruct((mesh_n,) + w.shape, bf) for w in (wq, wk, wv, wo)]
     out = pl.pallas_call(
-        functools.partial(attend_kernel, mesh_n, seq_len),
+        functools.partial(attend_kernel, mesh_n, stride, seq_len),
         in_specs=[vmem, hbm, hbm, hbm, hbm],
         out_specs=[vmem, hbm, hbm, hbm, hbm],
         out_shape=[jax.ShapeDtypeStruct((toks, dim), bf)] + fulls,
@@ -246,53 +269,25 @@
             pltpu.VMEM((toks, dim), bf),
             pltpu.VMEM((toks, width), bf),
             pltpu.VMEM((toks, width), bf),
-            pltpu.VMEM((toks, width), bf),
             pltpu.VMEM((2, mesh_n, wq.shape[0], min(512, width)), bf),
             pltpu.VMEM((2,) + wo.shape, bf),
             pltpu.VMEM((toks, dim), jnp.float32),
-            pltpu.SemaphoreType.DMA((4, 16)),
-            pltpu.SemaphoreType.DMA((4, 16)),
+            pltpu.SemaphoreType.DMA((4, 25)),
+            pltpu.SemaphoreType.DMA((4, 25)),
             pltpu.SemaphoreType.DMA((2,)),
         ],
-        compiler_params=pltpu.CompilerParams(collective_id=0, has_side_effects=True, vmem_limit_bytes=56 * 2 ** 20),
-        cost_estimate=pl.CostEstimate(flops=8 * toks * dim * width, bytes_accessed=200_000_000, transcendentals=0),
+        compiler_params=pltpu.CompilerParams(collective_id=0, has_side_effects=True, vmem_limit_bytes=VMEM_BYTES),
         name='attend',
     )(x, wq, wk, wv, wo)
     return out[0]
 
 
-def slot_table(ids_flat, experts):
-    tok_count = ids_flat.shape[0]
-    member = jnp.any(ids_flat[:, :, None] == jnp.arange(experts, dtype=jnp.int32), axis=1)
-    strict = lax.broadcasted_iota(jnp.int32, (tok_count, tok_count), 0) > lax.broadcasted_iota(jnp.int32, (tok_count, tok_count), 1)
-    before = jnp.dot(strict.astype(jnp.bfloat16), member.astype(jnp.bfloat16), preferred_element_type=jnp.float32)
-    return member, jnp.where(member, before.astype(jnp.int32), -1)
-
-
-def dense_gates(hidden, w_router, member):
-    normed = rms_norm(hidden)
-    logits = jnp.dot(normed, w_router, precision=lax.Precision.HIGHEST, preferred_element_type=jnp.float32)
-    top = jnp.max(jnp.where(member, logits, -jnp.inf), axis=1, keepdims=True)
-    grown = jnp.where(member, jnp.exp(jnp.where(member, logits, top) - top), 0.0)
-    return normed.astype(jnp.bfloat16), grown / jnp.sum(grown, axis=1, keepdims=True)
-
-
-def neighbours(mesh_n):
-    me = lax.axis_index('ep')
-    core = me % 2
-    sibling = me + 1 - 2 * core
-    return me, core, sibling, (me + 2) % mesh_n, (me + mesh_n - 2) % mesh_n, (me + mesh_n // 2) % mesh_n
-
-
-def meet(mesh_n, me):
-    barrier = pltpu.get_barrier_semaphore()
-    for j in range(1, mesh_n):
-        pl.semaphore_signal(barrier, inc=1, device_id={'ep': (me + j) % mesh_n}, device_id_type=MESH)
-    pl.semaphore_wait(barrier, mesh_n - 1)
-
-
-def route_kernel(mesh_n, u_ref, mine_ref, rows_ref, tab_ref, all_ref, hot_ref, stage_ref, send, recv, tab_send, tab_recv, out_sem):
+def route_kernel(mesh_n, h_ref, ids_ref, router_ref, rows_ref, tab_ref, need_ref, u_ref, z_ref, mine_ref, all_ref, hot_ref, stage_ref,
+                 send, recv, tab_send, tab_recv, out_sem):
     me, core, sibling, right, left, across = neighbours(mesh_n)
+    wide = h_ref[...].astype(jnp.float32)
+    z_ref[...] = wide * lax.rsqrt(jnp.mean(wide * wide, axis=-1, keepdims=True) + EPS)
+    u_ref[...] = z_ref[...].astype(jnp.bfloat16)
     meet(mesh_n, me)
     toks = u_ref.shape[0]
     half = toks // 2
@@ -340,16 +335,37 @@
         peer = (me + j) % mesh_n
         return table(j, mine_ref.at[peer], tab_ref.at[me], peer)
 
+    for slot in (0, 2, 1, 3, 6):
+        outgoing(slot).start()
+    experts = router_ref.shape[1]
+    owned = experts // mesh_n
+    index = lax.broadcasted_iota(jnp.int32, (experts, toks), 0)
+    member = index == ids_ref[0:1, :]
+    for j in range(1, ids_ref.shape[0]):
+        member = member | (index == ids_ref[j:j + 1, :])
+    earlier = lax.broadcasted_iota(jnp.int32, (toks, toks), 0) < lax.broadcasted_iota(jnp.int32, (toks, toks), 1)
+    rank = jnp.dot(jnp.where(member, 1.0, 0.0).astype(jnp.bfloat16), jnp.where(earlier, 1.0, 0.0).astype(jnp.bfloat16),
+                   preferred_element_type=jnp.float32)
+    slots = jnp.where(member, rank, -1.0)
+    logits = lax.dot_general(router_ref[...], z_ref[...], (((0,), (1,)), ((), ())), precision=lax.Precision.HIGHEST,
+                             preferred_element_type=jnp.float32)
+    top = jnp.max(jnp.where(member, logits, -jnp.inf), axis=0, keepdims=True)
+    grown = jnp.where(member, jnp.exp(jnp.where(member, logits, top) - top), 0.0)
+    gates = grown / jnp.sum(grown, axis=0, keepdims=True)
+    for j in range(mesh_n):
+        mine_ref[j, :owned] = slots[j * owned:(j + 1) * owned]
+        mine_ref[j, owned:] = gates[j * owned:(j + 1) * owned]
     for j in range(1, mesh_n):
         table_out(j).start()
-    for slot in (0, 2, 1, 3, 6):
-        outgoing(slot).start()
-    tab_ref[pl.ds(me, 1)] = mine_ref[pl.ds(me, 1)]
+    tab_ref[me] = mine_ref[me]
     for j in range(1, mesh_n):
         source = (me + mesh_n - j) % mesh_n
         table(j, tab_ref.at[source], tab_ref.at[source], source).wait_recv()
-
-    owned = tab_ref.shape[1] // 2
+    most = tab_ref[0, :owned]
+    for j in range(1, mesh_n):
+        most = jnp.maximum(most, tab_ref[j, :owned])
+    need_ref[...] = jnp.broadcast_to(jnp.max(most, axis=1, keepdims=True), need_ref.shape)
+
     parts = rows_ref.shape[1]
     cap = parts * SLOT
     dim = u_ref.shape[1]
@@ -360,14 +376,16 @@
         return pltpu.make_async_copy(stage_ref.at[k % 2], rows_ref.at[:, :, s], out_sem.at[k % 2])
 
     def send_rows(k, s, own=False):
-        pos = tab_ref[pl.ds(s, 1), :owned][0]
-        for e in range(owned):
-            hot_ref[e * cap:(e + 1) * cap, :] = jnp.where(lane == pos[e:e + 1, :], 1.0, 0.0).astype(jnp.bfloat16)
+        def mark(e, carry):
+            pos = tab_ref[s, pl.ds(e, 1)]
+            hot_ref[pl.ds(pl.multiple_of(e * cap, SLOT), cap), :] = jnp.where(lane == pos, 1.0, 0.0).astype(jnp.bfloat16)
+            return carry
+        lax.fori_loop(0, owned, mark, 0)
         if k >= 2:
             flush(k, s).wait()
         def part(c, carry):
             cols = pl.ds(pl.multiple_of(c * width, width), width)
-            block = u_ref[:, cols] if own else all_ref[pl.ds(s, 1), :, cols][0]
+            block = u_ref[:, cols] if own else all_ref[s, :, cols]
             rows = jnp.dot(hot_ref[...], block, preferred_element_type=jnp.float32).astype(jnp.bfloat16)
             stage_ref[k % 2, :, :, :, cols] = rows.reshape(owned, parts, SLOT, width)
             return carry
@@ -406,17 +424,24 @@
         outgoing(slot).wait_send()
 
 
-def route(mesh_n, u, table, parts):
-    toks, dim = u.shape
-    owned = table.shape[1] // 2
-    bf = jnp.bfloat16
+def route(mesh_n, h, ids, w_router, parts):
+    toks, dim = h.shape
+    owned = w_router.shape[1] // mesh_n
+    bf, f32 = jnp.bfloat16, jnp.float32
     vmem = pl.BlockSpec(memory_space=pltpu.VMEM)
     return pl.pallas_call(
         functools.partial(route_kernel, mesh_n),
-        in_specs=[vmem, vmem],
-        out_specs=[pl.BlockSpec(memory_space=pltpu.HBM), vmem],
-        out_shape=[jax.ShapeDtypeStruct((owned, parts, mesh_n, SLOT, dim), bf), jax.ShapeDtypeStruct(table.shape, jnp.float32)],
+        in_specs=[vmem, vmem, vmem],
+        out_specs=[pl.BlockSpec(memory_space=pltpu.HBM), vmem, vmem],
+        out_shape=[
+            jax.ShapeDtypeStruct((owned, parts, mesh_n, SLOT, dim), bf),
+            jax.ShapeDtypeStruct((mesh_n, 2 * owned, toks), f32),
+            jax.ShapeDtypeStruct((owned, 128), f32),
+        ],
         scratch_shapes=[
+            pltpu.VMEM((toks, dim), bf),
+            pltpu.VMEM((toks, dim), f32),
+            pltpu.VMEM((mesh_n, 2 * owned, toks), f32),
             pltpu.VMEM((mesh_n, toks, dim), bf),
             pltpu.VMEM((owned * parts * SLOT, toks), bf),
             pltpu.VMEM((2, owned, parts, SLOT, dim), bf),
@@ -426,10 +451,9 @@
             pltpu.SemaphoreType.DMA((mesh_n,)),
             pltpu.SemaphoreType.DMA((2,)),
         ],
-        compiler_params=pltpu.CompilerParams(collective_id=1, has_side_effects=True, vmem_limit_bytes=56 * 2 ** 20),
-        cost_estimate=pl.CostEstimate(flops=2 * mesh_n * owned * parts * SLOT * toks * dim, bytes_accessed=40_000_000, transcendentals=0),
+        compiler_params=pltpu.CompilerParams(collective_id=1, has_side_effects=True, vmem_limit_bytes=VMEM_BYTES),
         name='route',
-    )(u, table)
+    )(h, ids, w_router)
 
 
 def ffn_kernel(need_ref, rows_ref, one_ref, three_ref, two_ref, out_ref):
@@ -469,8 +493,7 @@
             out_specs=tile,
         ),
         out_shape=jax.ShapeDtypeStruct(rows.shape, jnp.bfloat16),
-        compiler_params=pltpu.CompilerParams(vmem_limit_bytes=60 * 2 ** 20),
-        cost_estimate=pl.CostEstimate(flops=6 * rows.size * inner, bytes_accessed=200_000_000, transcendentals=0),
+        compiler_params=pltpu.CompilerParams(vmem_limit_bytes=VMEM_BYTES),
         name="ffn",
     )(need, rows, w_one, w_three, w_two)
 
@@ -487,7 +510,6 @@
     cap = parts * SLOT
     width = min(512, dim)
     lane = lax.broadcasted_iota(jnp.int32, (cap, toks), 0).astype(jnp.float32)
-    over = (((0,), (0,)), ((), ()))
     chips = (across, right, left, me)
     jobs = [dest for chip in chips for dest in (chip + 1 - 2 * core, chip)]
 
@@ -495,24 +517,25 @@
         return pltpu.make_async_copy(done_ref.at[:, :, jobs[k]], load_ref.at[k % 2], load_sem.at[k % 2])
 
     def partial(k, out, index):
-        tab = tab_ref[pl.ds(jobs[k], 1)][0]
-        pos, gate = tab[:owned], tab[owned:]
-        big = gate.astype(jnp.bfloat16).astype(jnp.float32)
-        mid = (gate - big).astype(jnp.bfloat16).astype(jnp.float32)
-        low = (gate - big) - mid
-        for e in range(owned):
-            here = lane == pos[e:e + 1, :]
-            for ref, piece in ((big_ref, big), (mid_ref, mid), (low_ref, low)):
-                ref[e * cap:(e + 1) * cap, :] = jnp.where(here, piece[e:e + 1, :], 0.0).astype(jnp.bfloat16)
+        def mark(e, carry):
+            here = lane == tab_ref[jobs[k], pl.ds(e, 1)]
+            gate = tab_ref[jobs[k], pl.ds(owned + e, 1)]
+            big = gate.astype(jnp.bfloat16).astype(jnp.float32)
+            mid = (gate - big).astype(jnp.bfloat16).astype(jnp.float32)
+            rows = pl.ds(pl.multiple_of(e * cap, SLOT), cap)
+            for ref, piece in ((big_ref, big), (mid_ref, mid), (low_ref, (gate - big) - mid)):
+                ref[rows, :] = jnp.where(here, piece, 0.0).astype(jnp.bfloat16)
+            return carry
+        lax.fori_loop(0, owned, mark, 0)
         fetch(k).wait()
         if k + 1 < len(jobs):
             fetch(k + 1).start()
         def part(c, carry):
             cols = pl.ds(pl.multiple_of(c * width, width), width)
             block = load_ref[k % 2, :, :, :, cols].reshape(owned * cap, width)
-            total = lax.dot_general(low_ref[...], block, over, preferred_element_type=jnp.float32)
-            total += lax.dot_general(mid_ref[...], block, over, preferred_element_type=jnp.float32)
-            out[index, :, cols] = total + lax.dot_general(big_ref[...], block, over, preferred_element_type=jnp.float32)
+            total = lax.dot_general(low_ref[...], block, TALL_BY_TALL, preferred_element_type=jnp.float32)
+            total += lax.dot_general(mid_ref[...], block, TALL_BY_TALL, preferred_element_type=jnp.float32)
+            out[index, :, cols] = total + lax.dot_general(big_ref[...], block, TALL_BY_TALL, preferred_element_type=jnp.float32)
             return carry
         lax.fori_loop(0, dim // width, part, 0)
 
@@ -589,8 +612,7 @@
             pltpu.SemaphoreType.DMA((6,)),
             pltpu.SemaphoreType.DMA((6,)),
         ],
-        compiler_params=pltpu.CompilerParams(collective_id=2, has_side_effects=True, vmem_limit_bytes=60 * 2 ** 20),
-        cost_estimate=pl.CostEstimate(flops=6 * mesh_n * owned * parts * SLOT * toks * dim, bytes_accessed=60_000_000, transcendentals=0),
+        compiler_params=pltpu.CompilerParams(collective_id=2, has_side_effects=True, vmem_limit_bytes=VMEM_BYTES),
         name='settle',
     )(table, h, done)
 
@@ -599,6 +621,8 @@
     tok_spec = P(('dp', 'ep'))
     row_spec = P('ep')
     n = mesh.shape['ep']
+    places = [getattr(device, 'coords', None) for device in mesh.devices[:, 0]]
+    stride = mesh.shape['dp'] // 2 if places[0] is None else sum(place[1] == places[0][1] for place in places)
 
     def local_layer(tokens, w_query, w_key, w_value, w_out, w_router, w_one, w_three, w_two, expert_ids):
         seq_count, seq_len, model_dim = tokens.shape
@@ -608,13 +632,11 @@
         toks = seq_count * seq_len
         parts = 2 * toks * choices // experts // SLOT
 
-        member, slots = slot_table(expert_ids.reshape(toks, choices), experts)
         flat = [w.reshape(w.shape[0], -1) for w in (w_query, w_key, w_value, w_out)]
-        hidden = attend(n, seq_len, tokens.reshape(toks, model_dim), *flat)
-        normed, gates_local = dense_gates(hidden, w_router, member)
-        mine = jnp.concatenate([slots.astype(jnp.float32).T.reshape(n, owned, toks), gates_local.T.reshape(n, owned, toks)], axis=1)
-        rows, table = route(n, normed, mine, parts)
-        need = jnp.max(table[:, :owned], axis=(0, 2)).astype(jnp.int32) // SLOT + 1
+        hidden = attend(n, stride, seq_len, tokens.reshape(toks, model_dim), *flat)
+        ids = expert_ids.reshape(toks, choices).T
+        rows, table, most = route(n, hidden, ids, w_router, parts)
+        need = most[:, 0].astype(jnp.int32) // SLOT + 1
         done = ffn(need, rows, w_one, w_three, w_two)
         layer_out = settle(n, table, hidden, done)
         return layer_out.reshape(seq_count, seq_len, model_dim)

time: 571 us -> 483 us (0.85)
  Pallas kernels: 539 us -> 467 us
  other arithmetic: 7.94 us -> 1.34 us
    pallas_call x1, Pallas kernels: 277 us -> 198 us  [attend(): pl.pallas_call(functools.partial(attend_kernel, mesh_n, stride, seq_len),...]
    pallas_call x1, Pallas kernels: 68.6 us -> 77.7 us  [route(): pl.pallas_call(functools.partial(route_kernel, mesh_n), in_specs=[vmem, v...]
where the time goes in v4:
time: 483 us; the launch traced here: 482 us
  Pallas kernels  467 us (97%)
  local copies, waits for them, and re-layouts  12.9 us (3%)
    pallas_call x1, Pallas kernels, attend(): pl.pallas_call(functools.partial(attend_kernel, mesh_n, stride, seq_len),...  198 us
    pallas_call x1, Pallas kernels, settle(): pl.pallas_call(functools.partial(settle_kernel, mesh_n), in_specs=[vmem,...  120 us
    pallas_call x1, Pallas kernels, route(): pl.pallas_call(functools.partial(route_kernel, mesh_n), in_specs=[vmem, v...  77.7 us
    pallas_call x1, Pallas kernels, ffn(): pl.pallas_call(ffn_kernel, grid_spec=pltpu.PrefetchScalarGridSpec(num_sca...  70.9 us

profile of v4, /device:TPU:81, one launch (start us, length us, event | category | flops | bytes accessed | tf_op | source)
XLA Modules:
  0.0 481.5 jit_solution(12488295344677524509)
XLA Ops:
  0.0 0.0 copy-start
  0.0 0.0 copy-start.1
  0.0 4.1 copy.17
  4.1 0.0 copy-done
  4.1 0.0 copy-done.1
  4.1 6.1 %copy_bitcast_fusion = (bf16[256,4096]{1,0:T(8,128)(2,1)}, bf16[256,4096]{1,0:T(8,128)(2,1)}) fusion(bf16[32,8,32,128]{3,2,1,0:T(8,128)(2,1)S(1)} %bitcast.18, bf16[32,8,32,128]{3,2,1,0:T(8,128)(2,1)S(1)} %bitcast.19), kind=kLoop, calls=%fused_computation | loop fusion | bytes 8388608 | tf_op jit(solution)/shard_map/reshape | solution.py:635
  10.2 198.4 %attend.1 = (bf16[384,2048]{1,0:T(8,128)(2,1)}, bf16[8,256,4096]{2,1,0:T(8,128)(2,1)}, bf16[8,256,4096]{2,1,0:T(8,128)(2,1)}, bf16[8,256,4096]{2,1,0:T(8,128)(2,1)}, bf16[8,512,2048]{2,1,0:T(8,128)(2,1)}) custom-call(bf16[384,2048]{1,0:T(8,128)(2,1)} %bitcast.20, bf16[256,4096]{1,0:T(8,128)(2,1)} %bitcast.15, bf16[256,4096]{1,0:T(8,128)(2,1)} %get-tuple-element.14.wk_ref, ...), custom_call_target="tpu_custom_call" | custom-call | tf_op jit(solution)/shard_map/attend/pallas_call | solution.py:263
  208.6 77.7 %route.1 = (bf16[16,3,8,16,2048]{4,3,2,1,0:T(8,128)(2,1)}, f32[8,32,384]{2,1,0:T(8,128)}, f32[16,128]{1,0:T(8,128)}) custom-call(bf16[384,2048]{1,0:T(8,128)(2,1)} %get-tuple-element.9.h_ref, s32[8,384]{1,0:T(8,128)} %bitcast.21, f32[2048,128]{1,0:T(8,128)} %router_ref.1), custom_call_target="tpu_custom_call" | custom-call | tf_op jit(solution)/shard_map/route/pallas_call | solution.py:432
  286.3 0.8 convert_reduce_fusion
  287.2 0.5 fusion.need_ref
  287.7 70.9 %ffn.1.done_ref = bf16[16,3,8,16,2048]{4,3,2,1,0:T(8,128)(2,1)} custom-call(s32[16]{0:T(128)} %fusion.need_ref, bf16[16,3,8,16,2048]{4,3,2,1,0:T(8,128)(2,1)} %get-tuple-element.12.rows_ref, bf16[16,2048,768]{2,1,0:T(8,128)(2,1)} %one_ref.1, bf16[16,2048,768]{2,1,0:T(8,128)(2,1)} %three_ref.1, bf16[16,768,2048]{2,1,0:T(8,128)(2,1)} %two_ref.1), custom_call_target="tpu_custom_call" | custom-call | tf_op jit(solution)/shard_map/ffn/pallas_call | solution.py:482
  358.6 120.2 %settle.1 = bf16[384,2048]{1,0:T(8,128)(2,1)} custom-call(f32[8,32,384]{2,1,0:T(8,128)} %get-tuple-element.10.tab_ref, bf16[384,2048]{1,0:T(8,128)(2,1)} %get-tuple-element.9.h_ref, bf16[16,3,8,16,2048]{4,3,2,1,0:T(8,128)(2,1)} %ffn.1.done_ref), custom_call_target="tpu_custom_call" | custom-call | tf_op jit(solution)/shard_map/settle/pallas_call | solution.py:597
  478.8 2.7 copy.19
Async XLA Ops:
  0.0 4.1 copy-start
  0.0 4.1 copy-start.1

commit v5 on v4

--- a/solution.py
+++ b/solution.py
@@ -456,46 +456,82 @@
     )(h, ids, w_router)
 
 
-def ffn_kernel(need_ref, rows_ref, one_ref, three_ref, two_ref, out_ref):
-    parts, n = rows_ref.shape[1], rows_ref.shape[2]
-    dim = rows_ref.shape[4]
+def ffn_kernel(most_ref, rows_ref, one_ref, three_ref, two_ref, out_ref, in_buf, one_buf, three_buf, two_buf, out_buf, load_sem, part_sem, out_sem):
+    owned, parts, n, _, dim = rows_ref.shape
+    depth = one_buf.shape[0]
     step = n * SLOT
-    need = need_ref[pl.program_id(0)]
-    for used in range(parts + 1):
-        @pl.when(need == used)
+
+    def need(e):
+        return most_ref[e, 0].astype(jnp.int32) // SLOT + 1
+
+    def loads(e, act):
+        slot = e % depth
+        for i, (src, buf) in enumerate(((one_ref, one_buf), (three_ref, three_buf), (two_ref, two_buf))):
+            act(pltpu.make_async_copy(src.at[e], buf.at[slot], load_sem.at[slot, i]))
+        for p in range(parts):
+            @pl.when(p < need(e))
+            def _():
+                act(pltpu.make_async_copy(rows_ref.at[e, p], in_buf.at[slot, p], part_sem.at[slot, p]))
+
+    def store(e):
+        return pltpu.make_async_copy(out_buf.at[e % 2], out_ref.at[e], out_sem.at[e % 2])
+
+    def begin(copy):
+        copy.start()
+
+    def end(copy):
+        copy.wait()
+
+    for e in range(depth):
+        loads(e, begin)
+
+    def expert(e, carry):
+        slot, place, count = e % depth, e % 2, need(e)
+        loads(e, end)
+        @pl.when(e > 1)
         def _():
-            if used:
-                rows = rows_ref[0, :used].reshape(used * step, dim)
-                first = jnp.dot(rows, one_ref[0], preferred_element_type=jnp.float32)
-                third = jnp.dot(rows, three_ref[0], preferred_element_type=jnp.float32)
+            store(e).wait()
+        for used in range(1, parts + 1):
+            @pl.when(count == used)
+            def _():
+                rows = in_buf[slot, :used].reshape(used * step, dim)
+                first = jnp.dot(rows, one_buf[slot], preferred_element_type=jnp.float32)
+                third = jnp.dot(rows, three_buf[slot], preferred_element_type=jnp.float32)
                 acted = (jax.nn.silu(first) * third).astype(jnp.bfloat16)
-                done = jnp.dot(acted, two_ref[0], preferred_element_type=jnp.float32).astype(jnp.bfloat16)
-                out_ref[0, :used] = done.reshape(used, n, SLOT, dim)
-            if used < parts:
-                out_ref[0, used:] = jnp.zeros((parts - used, n, SLOT, dim), jnp.bfloat16)
-
-
-def ffn(need, rows, w_one, w_three, w_two):
+                done = jnp.dot(acted, two_buf[slot], preferred_element_type=jnp.float32).astype(jnp.bfloat16)
+                out_buf[place, :used] = done.reshape(used, n, SLOT, dim)
+                if used < parts:
+                    out_buf[place, used:] = jnp.zeros((parts - used, n, SLOT, dim), jnp.bfloat16)
+        store(e).start()
+        @pl.when(e + depth < owned)
+        def _():
+            loads(e + depth, begin)
+        return carry
+    lax.fori_loop(0, owned, expert, 0)
+    for e in range(owned - 2, owned):
+        store(e).wait()
+
+
+def ffn(most, rows, w_one, w_three, w_two):
     owned, parts, n, _, dim = rows.shape
-    inner = w_one.shape[2]
-    tile = pl.BlockSpec((1, parts, n, SLOT, dim), lambda e, _: (e, 0, 0, 0, 0))
+    depth = min(3, owned)
+    hbm = pl.BlockSpec(memory_space=pltpu.HBM)
     return pl.pallas_call(
         ffn_kernel,
-        grid_spec=pltpu.PrefetchScalarGridSpec(
-            num_scalar_prefetch=1,
-            grid=(owned,),
-            in_specs=[
-                tile,
-                pl.BlockSpec((1, dim, inner), lambda e, _: (e, 0, 0)),
-                pl.BlockSpec((1, dim, inner), lambda e, _: (e, 0, 0)),
-                pl.BlockSpec((1, inner, dim), lambda e, _: (e, 0, 0)),
-            ],
-            out_specs=tile,
-        ),
+        in_specs=[pl.BlockSpec(memory_space=pltpu.SMEM)] + [hbm] * 4,
+        out_specs=hbm,
         out_shape=jax.ShapeDtypeStruct(rows.shape, jnp.bfloat16),
+        scratch_shapes=[pltpu.VMEM((depth,) + rows.shape[1:], jnp.bfloat16)]
+        + [pltpu.VMEM((depth,) + w.shape[1:], jnp.bfloat16) for w in (w_one, w_three, w_two)]
+        + [
+            pltpu.VMEM((2,) + rows.shape[1:], jnp.bfloat16),
+            pltpu.SemaphoreType.DMA((depth, 3)),
+            pltpu.SemaphoreType.DMA((depth, parts)),
+            pltpu.SemaphoreType.DMA((2,)),
+        ],
         compiler_params=pltpu.CompilerParams(vmem_limit_bytes=VMEM_BYTES),
-        name="ffn",
-    )(need, rows, w_one, w_three, w_two)
+        name='ffn',
+    )(most, rows, w_one, w_three, w_two)
 
 
 def settle_kernel(mesh_n, tab_ref, h_ref, done_ref, y_ref, big_ref, mid_ref, low_ref, load_ref, pass_ref, twin_ref, sum_ref, far_ref, near_ref,
@@ -636,8 +672,7 @@
         hidden = attend(n, stride, seq_len, tokens.reshape(toks, model_dim), *flat)
         ids = expert_ids.reshape(toks, choices).T
         rows, table, most = route(n, hidden, ids, w_router, parts)
-        need = most[:, 0].astype(jnp.int32) // SLOT + 1
-        done = ffn(need, rows, w_one, w_three, w_two)
+        done = ffn(most, rows, w_one, w_three, w_two)
         layer_out = settle(n, table, hidden, done)
         return layer_out.reshape(seq_count, seq_len, model_dim)
 

time: 483 us -> 472 us (0.977)
  Pallas kernels: 467 us -> 459 us
    pallas_call x1, Pallas kernels: 70.9 us -> 63.2 us  [ffn(): pl.pallas_call(ffn_kernel, in_specs=[pl.BlockSpec(memory_space=pltpu.SMEM...]
where the time goes in v5:
time: 472 us
  Pallas kernels  459 us (97%)
  local copies, waits for them, and re-layouts  12.9 us (3%)
    pallas_call x1, Pallas kernels, attend(): pl.pallas_call(functools.partial(attend_kernel, mesh_n, stride, seq_len),...  198 us
    pallas_call x1, Pallas kernels, settle(): pl.pallas_call(functools.partial(settle_kernel, mesh_n), in_specs=[vmem,...  120 us
    pallas_call x1, Pallas kernels, route(): pl.pallas_call(functools.partial(route_kernel, mesh_n), in_specs=[vmem, v...  77.7 us
    pallas_call x1, Pallas kernels, ffn(): pl.pallas_call(ffn_kernel, in_specs=[pl.BlockSpec(memory_space=pltpu.SMEM...  63.2 us

profile of v5, /device:TPU:81, one launch (start us, length us, event | category | flops | bytes accessed | tf_op | source)
XLA Modules:
  0.0 472.5 jit_solution(12655688186353690016)
XLA Ops:
  0.0 0.0 copy-start
  0.0 0.0 copy-start.1
  0.0 4.1 copy.17
  4.1 0.0 copy-done
  4.1 0.0 copy-done.1
  4.1 6.1 %copy_bitcast_fusion = (bf16[256,4096]{1,0:T(8,128)(2,1)}, bf16[256,4096]{1,0:T(8,128)(2,1)}) fusion(bf16[32,8,32,128]{3,2,1,0:T(8,128)(2,1)S(1)} %bitcast.18, bf16[32,8,32,128]{3,2,1,0:T(8,128)(2,1)S(1)} %bitcast.19), kind=kLoop, calls=%fused_computation | loop fusion | bytes 8388608 | tf_op jit(solution)/shard_map/reshape | solution.py:671
  10.2 198.4 %attend.1 = (bf16[384,2048]{1,0:T(8,128)(2,1)}, bf16[8,256,4096]{2,1,0:T(8,128)(2,1)}, bf16[8,256,4096]{2,1,0:T(8,128)(2,1)}, bf16[8,256,4096]{2,1,0:T(8,128)(2,1)}, bf16[8,512,2048]{2,1,0:T(8,128)(2,1)}) custom-call(bf16[384,2048]{1,0:T(8,128)(2,1)} %bitcast.20, bf16[256,4096]{1,0:T(8,128)(2,1)} %bitcast.15, bf16[256,4096]{1,0:T(8,128)(2,1)} %get-tuple-element.14.wk_ref, ...), custom_call_target="tpu_custom_call" | custom-call | tf_op jit(solution)/shard_map/attend/pallas_call | solution.py:263
  208.6 77.7 %route.1 = (bf16[16,3,8,16,2048]{4,3,2,1,0:T(8,128)(2,1)}, f32[8,32,384]{2,1,0:T(8,128)}, f32[16,128]{1,0:T(8,128)}) custom-call(bf16[384,2048]{1,0:T(8,128)(2,1)} %get-tuple-element.9.h_ref, s32[8,384]{1,0:T(8,128)} %bitcast.21, f32[2048,128]{1,0:T(8,128)} %router_ref.1), custom_call_target="tpu_custom_call" | custom-call | tf_op jit(solution)/shard_map/route/pallas_call | solution.py:432
  286.3 63.2 %ffn.1.done_ref = bf16[16,3,8,16,2048]{4,3,2,1,0:T(8,128)(2,1)} custom-call(f32[16,128]{1,0:T(8,128)} %get-tuple-element.11.most_ref, bf16[16,3,8,16,2048]{4,3,2,1,0:T(8,128)(2,1)} %get-tuple-element.12.rows_ref, bf16[16,2048,768]{2,1,0:T(8,128)(2,1)} %one_ref.1, bf16[16,2048,768]{2,1,0:T(8,128)(2,1)} %three_ref.1, bf16[16,768,2048]{2,1,0:T(8,128)(2,1)} %two_ref.1), custom_call_target="tpu_custom_call" | custom-call | tf_op jit(solution)/shard_map/ffn/pallas_call | solution.py:519
  349.5 120.2 %settle.1 = bf16[384,2048]{1,0:T(8,128)(2,1)} custom-call(f32[8,32,384]{2,1,0:T(8,128)} %get-tuple-element.10.tab_ref, bf16[384,2048]{1,0:T(8,128)(2,1)} %get-tuple-element.9.h_ref, bf16[16,3,8,16,2048]{4,3,2,1,0:T(8,128)(2,1)} %ffn.1.done_ref), custom_call_target="tpu_custom_call" | custom-call | tf_op jit(solution)/shard_map/settle/pallas_call | solution.py:633
  469.7 2.7 copy.19
Async XLA Ops:
  0.0 4.1 copy-start
  0.0 4.1 copy-start.1

commit v6 on v5

--- a/solution.py
+++ b/solution.py
@@ -22,11 +22,13 @@
     return me, core, sibling, (me + 2) % mesh_n, (me + mesh_n - 2) % mesh_n, (me + mesh_n // 2) % mesh_n
 
 
-def meet(mesh_n, me):
-    barrier = pltpu.get_barrier_semaphore()
+def greet(mesh_n, me):
     for j in range(1, mesh_n):
-        pl.semaphore_signal(barrier, inc=1, device_id={'ep': (me + j) % mesh_n}, device_id_type=MESH)
-    pl.semaphore_wait(barrier, mesh_n - 1)
+        pl.semaphore_signal(pltpu.get_barrier_semaphore(), inc=1, device_id={'ep': (me + j) % mesh_n}, device_id_type=MESH)
+
+
+def meet(mesh_n):
+    pl.semaphore_wait(pltpu.get_barrier_semaphore(), mesh_n - 1)
 
 
 def attend_kernel(mesh_n, stride, seq_len, x_ref, wq_ref, wk_ref, wv_ref, wo_ref, h_ref, fq_ref, fk_ref, fv_ref, fo_ref,
@@ -285,10 +287,11 @@
 def route_kernel(mesh_n, h_ref, ids_ref, router_ref, rows_ref, tab_ref, need_ref, u_ref, z_ref, mine_ref, all_ref, hot_ref, stage_ref,
                  send, recv, tab_send, tab_recv, out_sem):
     me, core, sibling, right, left, across = neighbours(mesh_n)
+    greet(mesh_n, me)
     wide = h_ref[...].astype(jnp.float32)
     z_ref[...] = wide * lax.rsqrt(jnp.mean(wide * wide, axis=-1, keepdims=True) + EPS)
     u_ref[...] = z_ref[...].astype(jnp.bfloat16)
-    meet(mesh_n, me)
+    meet(mesh_n)
     toks = u_ref.shape[0]
     half = toks // 2
     lows, highs = pl.ds(0, half), pl.ds(half, half)
@@ -514,7 +517,7 @@
 
 def ffn(most, rows, w_one, w_three, w_two):
     owned, parts, n, _, dim = rows.shape
-    depth = min(3, owned)
+    depth = min(4, owned)
     hbm = pl.BlockSpec(memory_space=pltpu.HBM)
     return pl.pallas_call(
         ffn_kernel,
@@ -537,7 +540,7 @@
 def settle_kernel(mesh_n, tab_ref, h_ref, done_ref, y_ref, big_ref, mid_ref, low_ref, load_ref, pass_ref, twin_ref, sum_ref, far_ref, near_ref,
                   load_sem, twin_send, twin_recv, send, recv):
     me, core, sibling, right, left, across = neighbours(mesh_n)
-    meet(mesh_n, me)
+    greet(mesh_n, me)
     toks, dim = h_ref.shape
     half = toks // 2
     lows, highs = slice(0, half), slice(half, toks)
@@ -593,6 +596,8 @@
         if i >= 2:
             twin(i - 2).wait_send()
         partial(2 * i, pass_ref, i % 2)
+        if i == 0:
+            meet(mesh_n)
         twin(i).start()
         partial(2 * i + 1, sum_ref, i)
         twin(i).wait_recv()

time: 472 us -> 469 us (level)
  no operation moved by 1% of the time
where the time goes in v6:
time: 469 us; the launch traced here: 468 us
  Pallas kernels  455 us (97%)
  local copies, waits for them, and re-layouts  12.9 us (3%)
    pallas_call x1, Pallas kernels, attend(): pl.pallas_call(functools.partial(attend_kernel, mesh_n, stride, seq_len),...  198 us
    pallas_call x1, Pallas kernels, settle(): pl.pallas_call(functools.partial(settle_kernel, mesh_n), in_specs=[vmem,...  117 us
    pallas_call x1, Pallas kernels, route(): pl.pallas_call(functools.partial(route_kernel, mesh_n), in_specs=[vmem, v...  77 us
    pallas_call x1, Pallas kernels, ffn(): pl.pallas_call(ffn_kernel, in_specs=[pl.BlockSpec(memory_space=pltpu.SMEM...  62 us

profile of v6, /device:TPU:81, one launch (start us, length us, event | category | flops | bytes accessed | tf_op | source)
XLA Modules:
  0.0 467.8 jit_solution(8866005745932034424)
XLA Ops:
  0.0 0.0 copy-start
  0.0 0.0 copy-start.1
  0.0 4.1 copy.17
  4.1 0.0 copy-done
  4.1 0.0 copy-done.1
  4.1 6.1 %copy_bitcast_fusion = (bf16[256,4096]{1,0:T(8,128)(2,1)}, bf16[256,4096]{1,0:T(8,128)(2,1)}) fusion(bf16[32,8,32,128]{3,2,1,0:T(8,128)(2,1)S(1)} %bitcast.18, bf16[32,8,32,128]{3,2,1,0:T(8,128)(2,1)S(1)} %bitcast.19), kind=kLoop, calls=%fused_computation | loop fusion | bytes 8388608 | tf_op jit(solution)/shard_map/reshape | solution.py:676
  10.2 198.4 %attend.1 = (bf16[384,2048]{1,0:T(8,128)(2,1)}, bf16[8,256,4096]{2,1,0:T(8,128)(2,1)}, bf16[8,256,4096]{2,1,0:T(8,128)(2,1)}, bf16[8,256,4096]{2,1,0:T(8,128)(2,1)}, bf16[8,512,2048]{2,1,0:T(8,128)(2,1)}) custom-call(bf16[384,2048]{1,0:T(8,128)(2,1)} %bitcast.20, bf16[256,4096]{1,0:T(8,128)(2,1)} %bitcast.15, bf16[256,4096]{1,0:T(8,128)(2,1)} %get-tuple-element.14.wk_ref, ...), custom_call_target="tpu_custom_call" | custom-call | tf_op jit(solution)/shard_map/attend/pallas_call | solution.py:265
  208.6 77.0 %route.1 = (bf16[16,3,8,16,2048]{4,3,2,1,0:T(8,128)(2,1)}, f32[8,32,384]{2,1,0:T(8,128)}, f32[16,128]{1,0:T(8,128)}) custom-call(bf16[384,2048]{1,0:T(8,128)(2,1)} %get-tuple-element.9.h_ref, s32[8,384]{1,0:T(8,128)} %bitcast.21, f32[2048,128]{1,0:T(8,128)} %router_ref.1), custom_call_target="tpu_custom_call" | custom-call | tf_op jit(solution)/shard_map/route/pallas_call | solution.py:435
  285.6 62.0 %ffn.1.done_ref = bf16[16,3,8,16,2048]{4,3,2,1,0:T(8,128)(2,1)} custom-call(f32[16,128]{1,0:T(8,128)} %get-tuple-element.11.most_ref, bf16[16,3,8,16,2048]{4,3,2,1,0:T(8,128)(2,1)} %get-tuple-element.12.rows_ref, bf16[16,2048,768]{2,1,0:T(8,128)(2,1)} %one_ref.1, bf16[16,2048,768]{2,1,0:T(8,128)(2,1)} %three_ref.1, bf16[16,768,2048]{2,1,0:T(8,128)(2,1)} %two_ref.1), custom_call_target="tpu_custom_call" | custom-call | tf_op jit(solution)/shard_map/ffn/pallas_call | solution.py:522
  347.6 117.4 %settle.1 = bf16[384,2048]{1,0:T(8,128)(2,1)} custom-call(f32[8,32,384]{2,1,0:T(8,128)} %get-tuple-element.10.tab_ref, bf16[384,2048]{1,0:T(8,128)(2,1)} %get-tuple-element.9.h_ref, bf16[16,3,8,16,2048]{4,3,2,1,0:T(8,128)(2,1)} %ffn.1.done_ref), custom_call_target="tpu_custom_call" | custom-call | tf_op jit(solution)/shard_map/settle/pallas_call | solution.py:638
  465.0 2.7 copy.19
Async XLA Ops:
  0.0 4.1 copy-start
  0.0 4.1 copy-start.1
